TPU v7x, 32 devices: a whole 2x2x4 slice. The times are simulated.
32 devices in a mesh: member: 4 (over z), region: 8 (over y, x, core).
Axes of the slice: x: 2, y: 2, z: 4, core: 2. Of those that a mesh axis runs over, the one named last changes fastest.
Arguments:
- background: bfloat16 [64, 13, 192, 1024], P('member', None, 'region'), may hold values from -6 to 6
- obs_ens: bfloat16 [131072, 64], P(('member', 'region')), may hold values from -6 to 6
- obs_value: bfloat16 [131072], P(('member', 'region')), may hold values from -8 to 8
- obs_precision: bfloat16 [131072], P(('member', 'region')), may hold values from 0.0009994507 to 0.0099487305
- obs_row: int32 [131072], P(('member', 'region')), may hold values from 0 to 47
- obs_patch: int32 [131072, 1], P(('member', 'region')), may hold values from 0 to 31; in each aligned block of 4096 rows (0 to 4095, 4096 to 8191, ...) at most 256 rows name the same one
Outputs:
- analysis: bfloat16 [64, 13, 192, 1024], P(None, None, 'member', 'region')
Inputs may be any that keep to these rules, and one draw needn't show every extreme that they name: `obs_patch`: among the observations of one device, at most 256 fall in one patch, and some patch receives exactly 256 of them.
All inputs are finite; a program needn't handle non-finite values.
Results may differ from a plain program's by a relative error of at most 0.0015.
The roundings to bfloat16 on the way count: a program that leaves them out, or rounds other values in their place, can miss the bound.
Values may be sent and summed in bfloat16 or wider, within the bound.
A program may use at most 128 MiB of HBM per device.

v0:
```python
import functools
import math

import jax
import jax.numpy as jnp
from jax import lax
from jax.experimental import pallas as pl
from jax.experimental.pallas import tpu as pltpu
from jax.sharding import PartitionSpec as P


BAND = 2
NS_ITERS = 4
TILE = 8
LANES = 128
LATE = 3
EXTRAS = 8
MESH = pl.DeviceIdType.MESH


def exchange_kernel(
    members, regions, late, bg_ref, ens_ref, extras_ref, *refs
):
    strips = regions // members
    devices = members * regions
    channels = bg_ref.shape[1]
    early = channels - late
    recv_ref, own_ref = refs[:2]
    lift_refs = refs[2 : 1 + members]
    got_ref = refs[1 + members]
    (
        held_ref, packed_ref, extra_ref, rank_ref, obs_ref,
        local_sem, spread_send, spread_recv, lift_send, lift_recv, out_sem,
        in_sem, obs_sem,
    ) = refs[2 + members :]
    width, obs_rows = ens_ref.shape
    capacity = obs_ref.shape[2]
    m, r = lax.axis_index("member"), lax.axis_index("region")
    me = m * regions + r
    first_stage = members * strips

    ens_copy = pltpu.make_async_copy(ens_ref, packed_ref.at[0:width], in_sem.at[0])
    extra_copy = pltpu.make_async_copy(extras_ref, extra_ref, in_sem.at[1])
    ens_copy.start()
    extra_copy.start()
    barrier = pltpu.get_barrier_semaphore()

    def at_device(other):
        return {"member": lax.div(other, regions), "region": lax.rem(other, regions)}

    def greet(d, carry):
        other = lax.rem(me + d, devices)
        pl.semaphore_signal(
            barrier, inc=1, device_id=at_device(other), device_id_type=MESH
        )
        return carry

    lax.fori_loop(1, devices, greet, 0)
    pl.semaphore_wait(barrier, devices - 1)

    slot = jnp.where(lax.div(r, strips) == m, lax.rem(r, strips), first_stage + r)

    def block(c, b):
        return bg_ref.at[:, c, :, pl.ds(pl.multiple_of(b * LANES, LANES), LANES)]

    for c in range(channels):

        def spread(d, carry, c=c):
            b = lax.rem(r + d, regions)
            pltpu.make_async_remote_copy(
                block(c, b), held_ref.at[slot, c], spread_send.at[c], spread_recv.at[c],
                device_id={"region": b}, device_id_type=MESH,
            ).start()
            return carry

        lax.fori_loop(1, regions, spread, 0)
        pltpu.make_async_copy(block(c, r), held_ref.at[slot, c], local_sem.at[c]).start()

    lifted = (members - 1) * strips
    shifts = range(members - 1, 0, -1)

    def arrive(c):
        pltpu.make_async_copy(held_ref.at[0, c], held_ref.at[0, c], local_sem.at[c]).wait()
        spread_all = held_ref.at[0 : regions - 1, c]
        pltpu.make_async_copy(spread_all, spread_all, spread_recv.at[c]).wait()

    def forward(c):
        arrive(c)
        for s in shifts:
            a = lax.rem(m + s, members)
            for j in range(strips):
                pltpu.make_async_remote_copy(
                    held_ref.at[first_stage + a * strips + j, c],
                    held_ref.at[s * strips + j, c],
                    lift_send.at[c], lift_recv.at[c],
                    device_id={"member": a}, device_id_type=MESH,
                ).start()

    ens_copy.wait()
    extra_copy.wait()
    packed_ref[width:, :] = extra_ref[...].astype(jnp.bfloat16)
    chunk = math.gcd(obs_rows, 512)
    upper = (
        lax.broadcasted_iota(jnp.int32, (chunk, chunk), 0)
        < lax.broadcasted_iota(jnp.int32, (chunk, chunk), 1)
    ).astype(jnp.bfloat16)
    names = lax.broadcasted_iota(jnp.int32, (devices, 1), 0).astype(jnp.float32)
    offset = jnp.zeros((devices, 1), jnp.float32)
    for k in range(obs_rows // chunk):
        span = slice(k * chunk, (k + 1) * chunk)
        hit = extra_ref[3:4, span] == names
        one = hit.astype(jnp.float32)
        before = offset + jnp.dot(
            one.astype(jnp.bfloat16), upper, preferred_element_type=jnp.float32
        )
        rank_ref[:, span] = jnp.sum(jnp.where(hit, before, 0.0), axis=0, keepdims=True)
        offset = offset + jnp.sum(one, axis=1, keepdims=True)
    places = lax.broadcasted_iota(jnp.int32, (capacity, 1), 0).astype(jnp.float32)

    def place(d, carry):
        total = jnp.zeros((width + EXTRAS, capacity), jnp.float32)
        for k in range(obs_rows // chunk):
            span = slice(k * chunk, (k + 1) * chunk)
            mine = jnp.where(
                extra_ref[3:4, span] == d.astype(jnp.float32), rank_ref[:, span], -1.0
            )
            pick = (places == mine).astype(jnp.float32).astype(jnp.bfloat16)
            total = total + lax.dot_general(
                packed_ref[:, span], pick, (((1,), (1,)), ((), ())),
                preferred_element_type=jnp.float32,
            )
        obs_ref[d] = total.astype(jnp.bfloat16)
        return carry

    stages = min(4, early - 1)
    for k in range(stages):
        forward(k)
        lax.fori_loop(devices * k // stages, devices * (k + 1) // stages, place, 0)
    forward(stages)

    def send_obs(d, carry):
        other = lax.rem(me + d, devices)
        pltpu.make_async_remote_copy(
            obs_ref.at[other], got_ref.at[me], obs_sem.at[0], obs_sem.at[1],
            device_id=at_device(other), device_id_type=MESH,
        ).start()
        return carry

    lax.fori_loop(1, devices, send_obs, 0)
    pltpu.make_async_copy(obs_ref.at[me], got_ref.at[me], obs_sem.at[2]).start()
    for c in range(stages + 1, early):
        forward(c)

    def late_copies(c):
        copies = [pltpu.make_async_copy(held_ref.at[0:strips, c], own_ref.at[:, c - early], out_sem.at[c, 0])]
        for s in range(1, members):
            a = lax.rem(m + s, members)
            copies.append(
                pltpu.make_async_copy(
                    held_ref.at[pl.ds(first_stage + a * strips, strips), c],
                    lift_refs[s - 1].at[:, c - early],
                    out_sem.at[c, s],
                )
            )
        return copies

    for c in range(early, channels):
        arrive(c)
        for copy in late_copies(c):
            copy.start()

    def early_copy(c):
        return pltpu.make_async_copy(
            held_ref.at[0:first_stage, c], recv_ref.at[:, c], out_sem.at[c, 0]
        )

    for c in range(early):
        lift_all = held_ref.at[0:lifted, c]
        pltpu.make_async_copy(lift_all, lift_all, lift_recv.at[c]).wait()
        early_copy(c).start()
    for c in range(channels):
        spread_all = held_ref.at[0 : regions - 1, c]
        pltpu.make_async_copy(spread_all, spread_all, spread_send.at[c]).wait()
    obs_all = got_ref.at[0 : devices - 1]
    pltpu.make_async_copy(obs_all, obs_all, obs_sem.at[0]).wait()
    pltpu.make_async_copy(obs_all, obs_all, obs_sem.at[1]).wait()
    pltpu.make_async_copy(obs_ref.at[0], got_ref.at[0], obs_sem.at[2]).wait()
    for c in range(early, channels):
        for copy in late_copies(c):
            copy.wait()
    for c in range(early):
        lift_all = held_ref.at[0:lifted, c]
        pltpu.make_async_copy(lift_all, lift_all, lift_send.at[c]).wait()
        early_copy(c).wait()


def exchange(background, ens_cols, extras, capacity):
    members, regions = lax.axis_size("member"), lax.axis_size("region")
    strips = regions // members
    devices = members * regions
    local_members, channels, rows, _ = background.shape
    width, obs_rows = ens_cols.shape
    late = min(LATE, channels - 2)
    dma = pltpu.SemaphoreType.DMA
    kind = background.dtype
    part = jax.ShapeDtypeStruct((strips, late, local_members, rows, LANES), kind)
    out = pl.pallas_call(
        functools.partial(exchange_kernel, members, regions, late),
        in_specs=[pl.BlockSpec(memory_space=pl.ANY)] * 3,
        out_specs=[pl.BlockSpec(memory_space=pl.ANY)] * (members + 2),
        out_shape=[
            jax.ShapeDtypeStruct(
                (members * strips, channels - late, local_members, rows, LANES), kind
            )
        ]
        + [part] * members
        + [jax.ShapeDtypeStruct((devices, width + EXTRAS, capacity), jnp.bfloat16)],
        scratch_shapes=[
            pltpu.VMEM(
                (members * strips + regions, channels, local_members, rows, LANES), kind
            ),
            pltpu.VMEM((width + EXTRAS, obs_rows), jnp.bfloat16),
            pltpu.VMEM((EXTRAS, obs_rows), jnp.float32),
            pltpu.VMEM((1, obs_rows), jnp.float32),
            pltpu.VMEM((devices, width + EXTRAS, capacity), jnp.bfloat16),
        ]
        + [dma((channels,))] * 5
        + [dma((channels, members)), dma((2,)), dma((3,))],
        compiler_params=pltpu.CompilerParams(
            collective_id=0, has_side_effects=True, vmem_limit_bytes=60 << 20
        ),
        cost_estimate=pl.CostEstimate(
            flops=1 << 34, bytes_accessed=4 * background.size, transcendentals=0
        ),
    )(background, ens_cols, extras)
    return out[0], list(out[1 : 1 + members]), out[1 + members]


def gram_kernel(width, lat_rows, got_ref, gram_ref, proj_ref, scaled_ref):
    bands = lat_rows // BAND

    @pl.when(pl.program_id(0) == 0)
    def _():
        gram_ref[...] = jnp.zeros_like(gram_ref)
        proj_ref[...] = jnp.zeros_like(proj_ref)

    cols = jnp.concatenate(
        [got_ref[k].astype(jnp.float32) for k in range(got_ref.shape[0])], axis=1
    )
    ens = cols[:width]
    obs_val, obs_prec, row = (cols[width + k : width + k + 1] for k in range(3))
    mean = jnp.sum(ens, axis=0, keepdims=True) / width
    pert = (ens - mean).astype(jnp.bfloat16)
    pert_float = pert.astype(jnp.float32)
    innovation = obs_val - mean
    index = lax.broadcasted_iota(jnp.int32, (bands, 1), 0).astype(jnp.float32)
    distance = (row - (index * BAND + (BAND - 1) / 2.0)) / (lat_rows / 4.0)
    weight = obs_prec * jnp.exp(-0.5 * distance * distance)
    for j in range(bands):
        scaled_ref[j * width : (j + 1) * width, :] = (weight[j : j + 1] * pert_float).astype(
            jnp.bfloat16
        )
    over_obs = (((1,), (1,)), ((), ()))
    gram_ref[...] += lax.dot_general(
        scaled_ref[...], pert, over_obs, preferred_element_type=jnp.float32
    )
    proj_ref[...] += lax.dot_general(
        weight * innovation,
        pert_float,
        over_obs,
        precision=lax.Precision.HIGHEST,
        preferred_element_type=jnp.float32,
    )


def band_grams(got, width, lat_rows):
    devices, cols, capacity = got.shape
    bands = lat_rows // BAND
    group = max(1, math.gcd(devices, 1024 // capacity))
    gram, projected = pl.pallas_call(
        functools.partial(gram_kernel, width, lat_rows),
        grid=(devices // group,),
        in_specs=[pl.BlockSpec((group, cols, capacity), lambda i: (i, 0, 0))],
        out_specs=[
            pl.BlockSpec((bands * width, width), lambda i: (0, 0)),
            pl.BlockSpec((bands, width), lambda i: (0, 0)),
        ],
        out_shape=[
            jax.ShapeDtypeStruct((bands * width, width), jnp.float32),
            jax.ShapeDtypeStruct((bands, width), jnp.float32),
        ],
        scratch_shapes=[pltpu.VMEM((bands * width, group * capacity), jnp.bfloat16)],
        compiler_params=pltpu.CompilerParams(vmem_limit_bytes=24 << 20),
        cost_estimate=pl.CostEstimate(
            flops=8 * devices * capacity * bands * width * width,
            bytes_accessed=2 * devices * capacity * cols,
            transcendentals=devices * capacity * bands,
        ),
    )(got)
    return gram.reshape(bands, width, width), projected


def batched(left, right):
    return jnp.einsum("bij,bjk->bik", left, right, precision=lax.Precision.HIGHEST)


def band_transforms(grams, members):
    gram_band, projected = grams
    identity = jnp.eye(members, dtype=jnp.float32)
    system = (members - 1.0) * identity + gram_band
    norm_f = jnp.sqrt(jnp.sum(system * system, axis=(1, 2)))
    root_iter = system / norm_f[:, None, None]
    inv_root = jnp.broadcast_to(identity, system.shape)
    for _ in range(NS_ITERS):
        middle = 1.5 * identity - 0.5 * batched(inv_root, root_iter)
        root_iter = batched(root_iter, middle)
        inv_root = batched(middle, inv_root)
    spread = jnp.sqrt((members - 1.0) / norm_f)[:, None, None] * inv_root
    inverse = batched(inv_root, inv_root) / norm_f[:, None, None]
    mean_shift = jnp.einsum("bjk,bk->bj", inverse, projected, precision=lax.Precision.HIGHEST)
    return (spread + mean_shift[:, :, None]).astype(jnp.bfloat16)


def widen_kernel(transform_ref, wide_ref, turned_ref):
    bands, members, _, width = transform_ref.shape
    side = width * TILE
    m = lax.axis_index("member")
    for s in range(members):
        turned_ref[:, s] = transform_ref[:, lax.rem(m - s + members, members)]
    long = lax.broadcasted_iota(jnp.int32, (side, width), 0)
    repeat = (long // TILE == lax.broadcasted_iota(jnp.int32, (side, width), 1)).astype(
        jnp.bfloat16
    )
    row = lax.broadcasted_iota(jnp.int32, (side, side), 0) % TILE
    col = lax.broadcasted_iota(jnp.int32, (side, side), 1) % TILE
    same = row == col
    over_last = (((1,), (1,)), ((), ()))
    for t in range(bands * BAND // TILE):
        picked = jnp.zeros((side, width), jnp.float32)
        for j in range(TILE // BAND):
            band = turned_ref[t * (TILE // BAND) + j].reshape(width, width)
            tall = lax.dot_general(repeat, band, over_last, preferred_element_type=jnp.float32)
            picked = jnp.where(long % TILE // BAND == j, tall, picked)
        spread = lax.dot_general(
            picked.astype(jnp.bfloat16), repeat, over_last, preferred_element_type=jnp.float32
        )
        wide_ref[t] = jnp.where(same, spread, 0.0).astype(jnp.bfloat16)


def widen(transform, members):
    bands, width, _ = transform.shape
    side = width * TILE
    return pl.pallas_call(
        widen_kernel,
        in_specs=[pl.BlockSpec(memory_space=pltpu.VMEM)],
        out_specs=pl.BlockSpec(memory_space=pltpu.VMEM),
        out_shape=jax.ShapeDtypeStruct((bands * BAND // TILE, side, side), jnp.bfloat16),
        scratch_shapes=[pltpu.VMEM((bands, members, width // members, width), jnp.bfloat16)],
        compiler_params=pltpu.CompilerParams(vmem_limit_bytes=24 << 20),
        cost_estimate=pl.CostEstimate(
            flops=1 << 31, bytes_accessed=8 * side * side, transcendentals=0
        ),
    )(transform.reshape(bands, members, width // members, width))


def apply_kernel(members, pieces, wide_ref, *refs):
    parts, out_ref = refs[:pieces], refs[-1]
    slots, block, local_members, rows, lanes = parts[0].shape
    strips = slots * pieces // members
    width = members * local_members
    side = width * TILE
    tiles = rows // TILE
    for j in range(strips):
        for t in range(tiles):
            means, perts = [], []
            for c in range(block):
                states = []
                for s in range(members):
                    place = s * strips + j
                    ref = parts[place // slots]
                    states.append(
                        ref[place % slots, c, :, t * TILE : (t + 1) * TILE, :].astype(
                            jnp.float32
                        )
                    )
                state = jnp.concatenate(states, axis=0)
                mean = jnp.sum(state, axis=0) / width
                means.append(mean)
                perts.append((state - mean[None]).reshape(side, lanes).astype(jnp.bfloat16))
            gain = jnp.dot(
                wide_ref[j * tiles + t],
                jnp.concatenate(perts, axis=1),
                preferred_element_type=jnp.float32,
            )
            for c in range(block):
                one = gain[:, c * lanes : (c + 1) * lanes].reshape(width, TILE, lanes)
                first = j * rows + t * TILE
                out_ref[:, c, first : first + TILE, :] = (one + means[c][None]).astype(
                    jnp.bfloat16
                )


def apply_transform(parts, wide, members, channels, first, block, onto=None):
    slots, count, local_members, rows, lanes = parts[0].shape
    pieces = len(parts)
    strips = slots * pieces // members
    width = members * local_members
    operands = [wide, *parts]
    in_specs = [pl.BlockSpec(wide.shape, lambda i: (0, 0, 0))] + [
        pl.BlockSpec((slots, block, local_members, rows, lanes), lambda i: (0, i, 0, 0, 0))
    ] * pieces
    aliases = {}
    if onto is not None:
        aliases = {len(operands): 0}
        operands.append(onto)
        in_specs.append(pl.BlockSpec(memory_space=pl.ANY))
    skip = first // block
    return pl.pallas_call(
        functools.partial(apply_kernel, members, pieces),
        grid=(count // block,),
        in_specs=in_specs,
        out_specs=pl.BlockSpec(
            (width, block, strips * rows, lanes), lambda i: (0, i + skip, 0, 0)
        ),
        out_shape=jax.ShapeDtypeStruct((width, channels, strips * rows, lanes), jnp.bfloat16),
        input_output_aliases=aliases,
        compiler_params=pltpu.CompilerParams(vmem_limit_bytes=32 << 20),
        cost_estimate=pl.CostEstimate(
            flops=2 * width * count * strips * rows * lanes * width * TILE,
            bytes_accessed=4 * width * count * strips * rows * lanes,
            transcendentals=0,
        ),
    )(*operands)


def apply_plain(recv, late, transform, members):
    slots, _, local_members, rows, lanes = recv.shape
    strips = slots // members
    width = members * local_members
    states = jnp.concatenate([recv, jnp.concatenate(late, axis=0)], axis=1)
    channels = states.shape[1]
    states = states.reshape(members, strips, channels, local_members, rows, lanes)
    mean = jnp.sum(states, axis=(0, 3), dtype=jnp.float32) / width
    pert = (states.astype(jnp.float32) - mean[None, :, :, None]).astype(jnp.bfloat16)
    order = lax.rem(lax.axis_index("member") - jnp.arange(members) + members, members)
    gains = jnp.repeat(transform, BAND, axis=0).reshape(
        strips, rows, members, local_members, width
    )
    gains = jnp.take(gains, order, axis=2)
    gain = jnp.einsum(
        "mjcnxl,jxmnk->kcjxl", pert, gains, preferred_element_type=jnp.float32
    )
    out = mean.transpose(1, 0, 2, 3)[None] + gain
    return out.reshape(width, channels, strips * rows, lanes).astype(jnp.bfloat16)


def local(background, obs_ens, obs_value, obs_precision, obs_row, obs_patch):
    members = lax.axis_size("member")
    regions = lax.axis_size("region")
    obs_rows, width = obs_ens.shape
    capacity = 2 * obs_rows // (members * regions)
    rows = background.shape[2]
    channels = background.shape[1]
    lat_rows = (regions // members) * rows
    filler = jnp.zeros((obs_rows,), jnp.float32)
    columns = [obs_value, obs_precision, obs_row, obs_patch[:, 0]]
    extras = jnp.stack(
        [column.astype(jnp.float32) for column in columns] + [filler] * (EXTRAS - 4)
    )
    recv, late, got = exchange(background, obs_ens.T, extras, capacity)
    for shift in range(1, members):
        ring = [(k, (k + shift) % members) for k in range(members)]
        late[shift] = lax.ppermute(late[shift], "member", ring)
    grams = band_grams(got, width, lat_rows)
    transform = band_transforms(grams, width)
    if rows % TILE:
        return apply_plain(recv, late, transform, members)
    wide = widen(transform, members)
    early = recv.shape[1]
    out = apply_transform([recv], wide, members, channels, 0, math.gcd(early, 2))
    return apply_transform(late, wide, members, channels, early, 1, out)


def solution(mesh):
    in_specs = (
        P("member", None, "region", None),
        P(("member", "region"), None),
        P(("member", "region")),
        P(("member", "region")),
        P(("member", "region")),
        P(("member", "region"), None),
    )
    out_specs = P(None, None, "member", "region")
    return jax.shard_map(local, mesh=mesh, in_specs=in_specs, out_specs=out_specs, check_vma=False)
```

profile of v0, /device:TPU:11, one launch (start us, length us, event | category | flops | bytes accessed | tf_op | source)
XLA Modules:
  0.0 273.9 jit_solution(5746298921911038818)
XLA Ops:
  0.0 0.7 stack.29
  0.7 0.7 stack.30
  1.4 0.7 convert_element_type.26
  2.1 0.7 convert_bitcast_fusion
  2.9 0.8 stack.28.extras_ref
  3.6 209.7 %shard_map.64 = (bf16[8,10,16,24,128]{4,3,2,1,0:T(8,128)(2,1)}, bf16[2,3,16,24,128]{4,3,2,1,0:T(8,128)(2,1)}, bf16[2,3,16,24,128]{4,3,2,1,0:T(8,128)(2,1)}, bf16...) custom-call(bf16[16,13,24,1024]{3,2,1,0:T(8,128)(2,1)} %bg_ref.1, ...), custom_call_target="tpu_custom_call" | custom-call | flops 17179869184 | bytes 20447232 | tf_op jit(solution)/shard_map/pallas_call | solution.py:207
  213.4 2.9 %collective-permute-start = (bf16[2,3,16,24,128]{4,3,2,1,0:T(8,128)(2,1)}, bf16[2,3,16,24,128]{4,3,2,1,0:T(8,128)(2,1)S(1)}, u32[]{:S(2)}, u32[]{:S(2)}) collective-permute-start(bf16[2,3,16,24,128]{4,3,2,1,0:T(8,128)(2,1)} %get-tuple-element.17), channel_id=1, source_target_pairs={{0,8},{8,16},{16,24},{24,0},{1,9},{9,17},{17,25},{25,1},{2,10},{10... | collective-permute-start | bytes 1769480 | tf_op jit(solution)/shard_map/ppermute | solution.py:473
  216.2 2.2 collective-permute-start.1
  218.5 1.3 copy-done.1
  219.7 9.8 %shard_map.65 = (f32[1536,64]{1,0:T(8,128)S(1)}, f32[24,64]{1,0:T(8,128)S(1)}) custom-call(bf16[32,72,256]{2,1,0:T(8,128)(2,1)S(1)} %copy-done.1), custom_call_target="tpu_custom_call" | custom-call | flops 6442450944 | bytes 1179648 | tf_op jit(solution)/shard_map/pallas_call | solution.py:280
  229.5 0.3 fusion.5
  229.8 0.1 reduce_sum.14
  229.9 0.1 reduce_sum.18
  230.0 0.9 fusion.3
  230.9 1.0 fusion.9
  231.9 0.8 fusion.6
  232.7 0.9 fusion.2
  233.7 0.9 fusion.14
  234.6 0.9 fusion.13
  235.5 0.9 fusion.1
  236.4 0.9 fusion.15
  237.3 0.9 fusion.16
  238.3 0.9 fusion
  239.2 0.9 fusion.17
  240.1 0.9 convolution_divide_fusion
  241.0 1.5 fusion.18
  242.6 0.3 add_convert_fusion
  242.9 2.3 shard_map.66.wide_ref
  245.3 7.8 %shard_map.67.refs_4_ = bf16[64,13,48,128]{3,2,1,0:T(8,128)(2,1)} custom-call(bf16[6,512,512]{2,1,0:T(8,128)(2,1)S(1)} %shard_map.66.wide_ref, bf16[8,10,16,24,128]{4,3,2,1,0:T(8,128)(2,1)S(1)} %bitcast.42), custom_call_target="tpu_custom_call" | custom-call | flops 4026531840 | bytes 15728640 | tf_op jit(solution)/shard_map/pallas_call | solution.py:418
  253.0 14.4 %collective-permute-done.1.refs_2_ = bf16[2,3,16,24,128]{4,3,2,1,0:T(8,128)(2,1)S(1)} collective-permute-done((bf16[2,3,16,24,128]{4,3,2,1,0:T(8,128)(2,1)}, bf16[2,3,16,24,128]{4,3,2,1,0:T(8,128)(2,1)S(1)}, u32[]{:S(2)}, u32[]{:S(2)}) %collective-permute-start.1) | collective-permute-done | bytes 589856 | tf_op jit(solution)/shard_map/ppermute | solution.py:473
  267.4 2.1 collective-permute-done.2.refs_3_
  269.6 4.3 %shard_map.68 = bf16[64,13,48,128]{3,2,1,0:T(8,128)(2,1)} custom-call(bf16[6,512,512]{2,1,0:T(8,128)(2,1)S(1)} %shard_map.66.wide_ref, bf16[2,3,16,24,128]{4,3,2,1,0:T(8,128)(2,1)S(1)} %copy-done, bf16[2,3,16,24,128]{4,3,2,1,0:T(8,128)(2,1)S(1)} %collective-permute-done.refs_1_, ...), custom_call_target="tpu_custom_call", output_to_operand_aliasing={{}: (5, {})} | custom-call | flops 1207959552 | bytes 4718592 | tf_op jit(solution)/shard_map/pallas_call | solution.py:418
  (14 shorter events, 0.1 us)
Async XLA Ops:
  213.4 39.7 %collective-permute-start = (bf16[2,3,16,24,128]{4,3,2,1,0:T(8,128)(2,1)}, bf16[2,3,16,24,128]{4,3,2,1,0:T(8,128)(2,1)S(1)}, u32[]{:S(2)}, u32[]{:S(2)}) collective-permute-start(bf16[2,3,16,24,128]{4,3,2,1,0:T(8,128)(2,1)} %get-tuple-element.17), channel_id=1, source_target_pairs={{0,8},{8,16},{16,24},{24,0},{1,9},{9,17},{17,25},{25,1},{2,10},{10... | collective-permute-start | bytes 1769480 | tf_op jit(solution)/shard_map/ppermute | solution.py:473
  216.2 51.2 %collective-permute-start.1 = (bf16[2,3,16,24,128]{4,3,2,1,0:T(8,128)(2,1)}, bf16[2,3,16,24,128]{4,3,2,1,0:T(8,128)(2,1)S(1)}, u32[]{:S(2)}, u32[]{:S(2)}) collective-permute-start(bf16[2,3,16,24,128]{4,3,2,1,0:T(8,128)(2,1)} %get-tuple-element.18), channel_id=1, source_target_pairs={{0,16},{8,24},{16,0},{24,8},{1,17},{9,25},{17,1},{25,9},{2,18},{10... | collective-permute-start | bytes 1769480 | tf_op jit(solution)/shard_map/ppermute | solution.py:473
  218.4 51.2 %collective-permute-start.2 = (bf16[2,3,16,24,128]{4,3,2,1,0:T(8,128)(2,1)}, bf16[2,3,16,24,128]{4,3,2,1,0:T(8,128)(2,1)S(1)}, u32[]{:S(2)}, u32[]{:S(2)}) collective-permute-start(bf16[2,3,16,24,128]{4,3,2,1,0:T(8,128)(2,1)} %get-tuple-element.19), channel_id=1, source_target_pairs={{0,24},{8,0},{16,8},{24,16},{1,25},{9,1},{17,9},{25,17},{2,26},{10... | collective-permute-start | bytes 1769480 | tf_op jit(solution)/shard_map/ppermute | solution.py:473
  218.4 1.3 copy-start.1
  237.3 7.9 %slice-start = ((s8[7864320]{0:T(1024)(128)(4,1)}), s8[4194304]{0:T(1024)(128)(4,1)S(1)}, s32[]{:S(2)}) async-start(s8[7864320]{0:T(1024)(128)(4,1)} %bitcast.41), calls=%async_computation | async-start | bytes 8388608
  241.0 4.2 %slice-start.1 = ((s8[7864320]{0:T(1024)(128)(4,1)}), s8[3670016]{0:T(1024)(128)(4,1)S(1)}, s32[]{:S(2)}) async-start(s8[7864320]{0:T(1024)(128)(4,1)} %bitcast.41), calls=%async_computation.1 | async-start | bytes 7340032
  245.3 24.3 %copy-start = (bf16[2,3,16,24,128]{4,3,2,1,0:T(8,128)(2,1)S(1)}, bf16[2,3,16,24,128]{4,3,2,1,0:T(8,128)(2,1)}, u32[]{:S(2)}) copy-start(bf16[2,3,16,24,128]{4,3,2,1,0:T(8,128)(2,1)} %get-tuple-element.16.refs_0_) | copy-start | bytes 1769476
where the time goes:
time: 274 us
  Pallas kernels  234 us (85%)
  waiting for transfers between devices  16.5 us (6%)
  matrix products  12.4 us (5%)
  starting transfers between devices  5.05 us (2%)
  other arithmetic  3.58 us (1%)
    pallas_call x1, Pallas kernels, exchange(): pl.pallas_call(functools.partial(exchange_kernel, members, regions, late)...  210 us
    ppermute x3, waiting for transfers between devices, local(): late[shift] = lax.ppermute(late[shift], 'member', ring)  16.5 us
    pallas_call x2, Pallas kernels, apply_transform(): pl.pallas_call(functools.partial(apply_kernel, members, pieces), grid=(co...  12.1 us
    dot_general x12, matrix products, batched(): jnp.einsum('bij,bjk->bik', left, right, precision=lax.Precision.HIGHEST)  10.9 us
    pallas_call x1, Pallas kernels, band_grams(): pl.pallas_call(functools.partial(gram_kernel, width, lat_rows), grid=(dev...  9.8 us
  transfers between devices with their start and end apart: 3, of which 2 were waited for; matrix products, arithmetic and copies ran while one was open for 5% of the time, Pallas kernels for 7%

commit v1 on v0

--- a/solution.py
+++ b/solution.py
@@ -13,23 +13,22 @@
 NS_ITERS = 4
 TILE = 8
 LANES = 128
-LATE = 3
+LATE = 2
 EXTRAS = 8
 MESH = pl.DeviceIdType.MESH
 
 
 def exchange_kernel(
-    members, regions, late, bg_ref, ens_ref, extras_ref, *refs
+    members, regions, late, bg_ref, ens_ref, value_ref, precision_ref, row_ref, patch_ref, *refs
 ):
     strips = regions // members
     devices = members * regions
     channels = bg_ref.shape[1]
-    early = channels - late
     recv_ref, own_ref = refs[:2]
     lift_refs = refs[2 : 1 + members]
     got_ref = refs[1 + members]
     (
-        held_ref, packed_ref, extra_ref, rank_ref, obs_ref,
+        held_ref, packed_ref, pair_ref, whole_ref, extra_ref, rank_ref, obs_ref,
         local_sem, spread_send, spread_recv, lift_send, lift_recv, out_sem,
         in_sem, obs_sem,
     ) = refs[2 + members :]
@@ -37,12 +36,19 @@
     capacity = obs_ref.shape[2]
     m, r = lax.axis_index("member"), lax.axis_index("region")
     me = m * regions + r
+    home, seat = lax.div(r, strips), lax.rem(r, strips)
     first_stage = members * strips
-
-    ens_copy = pltpu.make_async_copy(ens_ref, packed_ref.at[0:width], in_sem.at[0])
-    extra_copy = pltpu.make_async_copy(extras_ref, extra_ref, in_sem.at[1])
-    ens_copy.start()
-    extra_copy.start()
+    order = list(range(late, channels)) + list(range(late))
+
+    copies_in = [
+        pltpu.make_async_copy(ens_ref, packed_ref.at[0:width], in_sem.at[0]),
+        pltpu.make_async_copy(value_ref, pair_ref.at[0], in_sem.at[1]),
+        pltpu.make_async_copy(precision_ref, pair_ref.at[1], in_sem.at[2]),
+        pltpu.make_async_copy(row_ref, whole_ref.at[0], in_sem.at[3]),
+        pltpu.make_async_copy(patch_ref, whole_ref.at[1], in_sem.at[4]),
+    ]
+    for copy in copies_in:
+        copy.start()
     barrier = pltpu.get_barrier_semaphore()
 
     def at_device(other):
@@ -58,36 +64,47 @@
     lax.fori_loop(1, devices, greet, 0)
     pl.semaphore_wait(barrier, devices - 1)
 
-    slot = jnp.where(lax.div(r, strips) == m, lax.rem(r, strips), first_stage + r)
+    slot = jnp.where(home == m, seat, first_stage + r)
+    groups = [0] + sorted(range(1, members), key=lambda g: (abs(2 * g - members), g))
 
     def block(c, b):
         return bg_ref.at[:, c, :, pl.ds(pl.multiple_of(b * LANES, LANES), LANES)]
 
-    for c in range(channels):
-
-        def spread(d, carry, c=c):
-            b = lax.rem(r + d, regions)
-            pltpu.make_async_remote_copy(
-                block(c, b), held_ref.at[slot, c], spread_send.at[c], spread_recv.at[c],
-                device_id={"region": b}, device_id_type=MESH,
-            ).start()
-            return carry
-
-        lax.fori_loop(1, regions, spread, 0)
+    def spread(c, b):
+        pltpu.make_async_remote_copy(
+            block(c, b), held_ref.at[slot, c], spread_send.at[c], spread_recv.at[c, home],
+            device_id={"region": b}, device_id_type=MESH,
+        ).start()
+
+    for c in order:
         pltpu.make_async_copy(block(c, r), held_ref.at[slot, c], local_sem.at[c]).start()
+        for j in range(1, strips):
+            spread(c, home * strips + lax.rem(seat + j, strips))
+        for g in groups[1:]:
+
+            def spread_group(j, carry, c=c, g=g):
+                spread(c, lax.rem(home + g, members) * strips + j)
+                return carry
+
+            lax.fori_loop(0, strips, spread_group, 0)
 
     lifted = (members - 1) * strips
-    shifts = range(members - 1, 0, -1)
-
-    def arrive(c):
-        pltpu.make_async_copy(held_ref.at[0, c], held_ref.at[0, c], local_sem.at[c]).wait()
-        spread_all = held_ref.at[0 : regions - 1, c]
-        pltpu.make_async_copy(spread_all, spread_all, spread_recv.at[c]).wait()
-
-    def forward(c):
-        arrive(c)
-        for s in shifts:
-            a = lax.rem(m + s, members)
+
+    def arrive(c, g):
+        a = lax.rem(home + g, members)
+        if g == 0:
+            pltpu.make_async_copy(held_ref.at[0, c], held_ref.at[0, c], local_sem.at[c]).wait()
+        if g or strips > 1:
+            some = held_ref.at[0 : strips if g else strips - 1, c]
+            pltpu.make_async_copy(some, some, spread_recv.at[c, a]).wait()
+        return a
+
+    def forward(c, g):
+        a = arrive(c, g)
+        s = lax.rem(a - m + members, members)
+
+        @pl.when(a != m)
+        def _():
             for j in range(strips):
                 pltpu.make_async_remote_copy(
                     held_ref.at[first_stage + a * strips + j, c],
@@ -96,8 +113,24 @@
                     device_id={"member": a}, device_id_type=MESH,
                 ).start()
 
-    ens_copy.wait()
-    extra_copy.wait()
+    early = order[: channels - late]
+    ahead = early[: min(3, len(early))]
+    for c in ahead:
+        forward(c, 0)
+
+    def forward_rest(c):
+        for g in groups:
+            if g or c not in ahead:
+                forward(c, g)
+
+    for copy in copies_in:
+        copy.wait()
+    obs_lines = obs_rows // LANES
+    for k, lines in enumerate([pair_ref[0], pair_ref[1], whole_ref[0], whole_ref[1]]):
+        lines = lines.astype(jnp.float32)
+        for i in range(obs_lines):
+            extra_ref[k : k + 1, i * LANES : (i + 1) * LANES] = lines[i : i + 1]
+    extra_ref[4:, :] = jnp.zeros((EXTRAS - 4, obs_rows), jnp.float32)
     packed_ref[width:, :] = extra_ref[...].astype(jnp.bfloat16)
     chunk = math.gcd(obs_rows, 512)
     upper = (
@@ -132,11 +165,11 @@
         obs_ref[d] = total.astype(jnp.bfloat16)
         return carry
 
-    stages = min(4, early - 1)
+    stages = min(4, len(early) - 1)
     for k in range(stages):
-        forward(k)
+        forward_rest(early[k])
         lax.fori_loop(devices * k // stages, devices * (k + 1) // stages, place, 0)
-    forward(stages)
+    forward_rest(early[stages])
 
     def send_obs(d, carry):
         other = lax.rem(me + d, devices)
@@ -148,33 +181,36 @@
 
     lax.fori_loop(1, devices, send_obs, 0)
     pltpu.make_async_copy(obs_ref.at[me], got_ref.at[me], obs_sem.at[2]).start()
-    for c in range(stages + 1, early):
-        forward(c)
+    for c in early[stages + 1 :]:
+        forward_rest(c)
 
     def late_copies(c):
-        copies = [pltpu.make_async_copy(held_ref.at[0:strips, c], own_ref.at[:, c - early], out_sem.at[c, 0])]
+        copies = [
+            pltpu.make_async_copy(held_ref.at[0:strips, c], own_ref.at[:, c], out_sem.at[c, 0])
+        ]
         for s in range(1, members):
             a = lax.rem(m + s, members)
             copies.append(
                 pltpu.make_async_copy(
                     held_ref.at[pl.ds(first_stage + a * strips, strips), c],
-                    lift_refs[s - 1].at[:, c - early],
+                    lift_refs[s - 1].at[:, c],
                     out_sem.at[c, s],
                 )
             )
         return copies
 
-    for c in range(early, channels):
-        arrive(c)
+    for c in range(late):
+        for g in groups:
+            arrive(c, g)
         for copy in late_copies(c):
             copy.start()
 
     def early_copy(c):
         return pltpu.make_async_copy(
-            held_ref.at[0:first_stage, c], recv_ref.at[:, c], out_sem.at[c, 0]
+            held_ref.at[0:first_stage, c], recv_ref.at[:, c - late], out_sem.at[c, 0]
         )
 
-    for c in range(early):
+    for c in early:
         lift_all = held_ref.at[0:lifted, c]
         pltpu.make_async_copy(lift_all, lift_all, lift_recv.at[c]).wait()
         early_copy(c).start()
@@ -185,28 +221,29 @@
     pltpu.make_async_copy(obs_all, obs_all, obs_sem.at[0]).wait()
     pltpu.make_async_copy(obs_all, obs_all, obs_sem.at[1]).wait()
     pltpu.make_async_copy(obs_ref.at[0], got_ref.at[0], obs_sem.at[2]).wait()
-    for c in range(early, channels):
+    for c in range(late):
         for copy in late_copies(c):
             copy.wait()
-    for c in range(early):
+    for c in early:
         lift_all = held_ref.at[0:lifted, c]
         pltpu.make_async_copy(lift_all, lift_all, lift_send.at[c]).wait()
         early_copy(c).wait()
 
 
-def exchange(background, ens_cols, extras, capacity):
+def exchange(background, ens_cols, lines, capacity):
     members, regions = lax.axis_size("member"), lax.axis_size("region")
     strips = regions // members
     devices = members * regions
     local_members, channels, rows, _ = background.shape
     width, obs_rows = ens_cols.shape
+    obs_lines = obs_rows // LANES
     late = min(LATE, channels - 2)
     dma = pltpu.SemaphoreType.DMA
     kind = background.dtype
     part = jax.ShapeDtypeStruct((strips, late, local_members, rows, LANES), kind)
     out = pl.pallas_call(
         functools.partial(exchange_kernel, members, regions, late),
-        in_specs=[pl.BlockSpec(memory_space=pl.ANY)] * 3,
+        in_specs=[pl.BlockSpec(memory_space=pl.ANY)] * 6,
         out_specs=[pl.BlockSpec(memory_space=pl.ANY)] * (members + 2),
         out_shape=[
             jax.ShapeDtypeStruct(
@@ -220,19 +257,23 @@
                 (members * strips + regions, channels, local_members, rows, LANES), kind
             ),
             pltpu.VMEM((width + EXTRAS, obs_rows), jnp.bfloat16),
+            pltpu.VMEM((2, obs_lines, LANES), jnp.bfloat16),
+            pltpu.VMEM((2, obs_lines, LANES), jnp.int32),
             pltpu.VMEM((EXTRAS, obs_rows), jnp.float32),
             pltpu.VMEM((1, obs_rows), jnp.float32),
             pltpu.VMEM((devices, width + EXTRAS, capacity), jnp.bfloat16),
         ]
-        + [dma((channels,))] * 5
-        + [dma((channels, members)), dma((2,)), dma((3,))],
+        + [dma((channels,))] * 2
+        + [dma((channels, members))]
+        + [dma((channels,))] * 2
+        + [dma((channels, members)), dma((5,)), dma((3,))],
         compiler_params=pltpu.CompilerParams(
             collective_id=0, has_side_effects=True, vmem_limit_bytes=60 << 20
         ),
         cost_estimate=pl.CostEstimate(
             flops=1 << 34, bytes_accessed=4 * background.size, transcendentals=0
         ),
-    )(background, ens_cols, extras)
+    )(background, ens_cols, *lines)
     return out[0], list(out[1 : 1 + members]), out[1 + members]
 
 
@@ -363,81 +404,120 @@
     )(transform.reshape(bands, members, width // members, width))
 
 
-def apply_kernel(members, pieces, wide_ref, *refs):
-    parts, out_ref = refs[:pieces], refs[-1]
-    slots, block, local_members, rows, lanes = parts[0].shape
-    strips = slots * pieces // members
+def tile_gain(parts, wide_ref, members, j, t, block):
+    slots, _, local_members, rows, lanes = parts[0].shape
+    strips = slots * len(parts) // members
     width = members * local_members
-    side = width * TILE
-    tiles = rows // TILE
-    for j in range(strips):
-        for t in range(tiles):
-            means, perts = [], []
-            for c in range(block):
-                states = []
-                for s in range(members):
-                    place = s * strips + j
-                    ref = parts[place // slots]
-                    states.append(
-                        ref[place % slots, c, :, t * TILE : (t + 1) * TILE, :].astype(
-                            jnp.float32
-                        )
-                    )
-                state = jnp.concatenate(states, axis=0)
-                mean = jnp.sum(state, axis=0) / width
-                means.append(mean)
-                perts.append((state - mean[None]).reshape(side, lanes).astype(jnp.bfloat16))
-            gain = jnp.dot(
-                wide_ref[j * tiles + t],
-                jnp.concatenate(perts, axis=1),
-                preferred_element_type=jnp.float32,
+    means, perts = [], []
+    for c in range(block):
+        states = []
+        for s in range(members):
+            place = s * strips + j
+            states.append(
+                parts[place // slots][
+                    place % slots, c, :, t * TILE : (t + 1) * TILE, :
+                ].astype(jnp.float32)
             )
-            for c in range(block):
-                one = gain[:, c * lanes : (c + 1) * lanes].reshape(width, TILE, lanes)
-                first = j * rows + t * TILE
-                out_ref[:, c, first : first + TILE, :] = (one + means[c][None]).astype(
-                    jnp.bfloat16
-                )
-
-
-def apply_transform(parts, wide, members, channels, first, block, onto=None):
-    slots, count, local_members, rows, lanes = parts[0].shape
-    pieces = len(parts)
-    strips = slots * pieces // members
+        state = jnp.concatenate(states, axis=0)
+        mean = jnp.sum(state, axis=0) / width
+        means.append(mean)
+        perts.append((state - mean[None]).reshape(width * TILE, lanes).astype(jnp.bfloat16))
+    gain = jnp.dot(
+        wide_ref[j * (rows // TILE) + t],
+        jnp.concatenate(perts, axis=1),
+        preferred_element_type=jnp.float32,
+    )
+    return [
+        (
+            gain[:, c * lanes : (c + 1) * lanes].reshape(width, TILE, lanes) + means[c][None]
+        ).astype(jnp.bfloat16)
+        for c in range(block)
+    ]
+
+
+def apply_kernel(members, wide_ref, part_ref, out_ref):
+    slots, block, _, rows, _ = part_ref.shape
+    for j in range(slots // members):
+        for t in range(rows // TILE):
+            first = j * rows + t * TILE
+            for c, value in enumerate(tile_gain([part_ref], wide_ref, members, j, t, block)):
+                out_ref[:, c, first : first + TILE, :] = value
+
+
+def apply_early(part, wide, members, channels, block):
+    slots, count, local_members, rows, lanes = part.shape
+    strips = slots // members
     width = members * local_members
-    operands = [wide, *parts]
-    in_specs = [pl.BlockSpec(wide.shape, lambda i: (0, 0, 0))] + [
-        pl.BlockSpec((slots, block, local_members, rows, lanes), lambda i: (0, i, 0, 0, 0))
-    ] * pieces
-    aliases = {}
-    if onto is not None:
-        aliases = {len(operands): 0}
-        operands.append(onto)
-        in_specs.append(pl.BlockSpec(memory_space=pl.ANY))
-    skip = first // block
+    skip = (channels - count) // block
     return pl.pallas_call(
-        functools.partial(apply_kernel, members, pieces),
-        grid=(count // block,),
-        in_specs=in_specs,
+        functools.partial(apply_kernel, members),
+        grid=(pl.cdiv(count, block),),
+        in_specs=[
+            pl.BlockSpec(wide.shape, lambda i: (0, 0, 0)),
+            pl.BlockSpec((slots, block, local_members, rows, lanes), lambda i: (0, i, 0, 0, 0)),
+        ],
         out_specs=pl.BlockSpec(
             (width, block, strips * rows, lanes), lambda i: (0, i + skip, 0, 0)
         ),
         out_shape=jax.ShapeDtypeStruct((width, channels, strips * rows, lanes), jnp.bfloat16),
-        input_output_aliases=aliases,
         compiler_params=pltpu.CompilerParams(vmem_limit_bytes=32 << 20),
         cost_estimate=pl.CostEstimate(
             flops=2 * width * count * strips * rows * lanes * width * TILE,
             bytes_accessed=4 * width * count * strips * rows * lanes,
             transcendentals=0,
         ),
-    )(*operands)
+    )(wide, part)
+
+
+def late_kernel(members, wide_ref, *refs):
+    parts, (out_ref, done_ref, sem) = refs[:members], refs[members + 1 :]
+    strips, block, _, rows, _ = parts[0].shape
+    copies = []
+    for j in range(strips):
+        for t in range(rows // TILE):
+            k = j * (rows // TILE) + t
+            for c, value in enumerate(tile_gain(parts, wide_ref, members, j, t, block)):
+                done_ref[k, :, c] = value
+            copy = pltpu.make_async_copy(
+                done_ref.at[k],
+                out_ref.at[:, 0:block, pl.ds(j * rows + t * TILE, TILE), :],
+                sem.at[k],
+            )
+            copy.start()
+            copies.append(copy)
+    for copy in copies:
+        copy.wait()
+
+
+def apply_late(parts, wide, members, onto):
+    strips, block, local_members, rows, lanes = parts[0].shape
+    width = members * local_members
+    tiles = strips * rows // TILE
+    return pl.pallas_call(
+        functools.partial(late_kernel, members),
+        in_specs=[pl.BlockSpec(memory_space=pltpu.VMEM)] * (1 + members)
+        + [pl.BlockSpec(memory_space=pl.ANY)],
+        out_specs=pl.BlockSpec(memory_space=pl.ANY),
+        out_shape=jax.ShapeDtypeStruct(onto.shape, onto.dtype),
+        input_output_aliases={1 + members: 0},
+        scratch_shapes=[
+            pltpu.VMEM((tiles, width, block, TILE, lanes), jnp.bfloat16),
+            pltpu.SemaphoreType.DMA((tiles,)),
+        ],
+        compiler_params=pltpu.CompilerParams(vmem_limit_bytes=32 << 20),
+        cost_estimate=pl.CostEstimate(
+            flops=2 * width * block * strips * rows * lanes * width * TILE,
+            bytes_accessed=4 * width * block * strips * rows * lanes,
+            transcendentals=0,
+        ),
+    )(wide, *parts, onto)
 
 
 def apply_plain(recv, late, transform, members):
     slots, _, local_members, rows, lanes = recv.shape
     strips = slots // members
     width = members * local_members
-    states = jnp.concatenate([recv, jnp.concatenate(late, axis=0)], axis=1)
+    states = jnp.concatenate([jnp.concatenate(late, axis=0), recv], axis=1)
     channels = states.shape[1]
     states = states.reshape(members, strips, channels, local_members, rows, lanes)
     mean = jnp.sum(states, axis=(0, 3), dtype=jnp.float32) / width
@@ -462,12 +542,11 @@
     rows = background.shape[2]
     channels = background.shape[1]
     lat_rows = (regions // members) * rows
-    filler = jnp.zeros((obs_rows,), jnp.float32)
-    columns = [obs_value, obs_precision, obs_row, obs_patch[:, 0]]
-    extras = jnp.stack(
-        [column.astype(jnp.float32) for column in columns] + [filler] * (EXTRAS - 4)
-    )
-    recv, late, got = exchange(background, obs_ens.T, extras, capacity)
+    lines = [
+        column.reshape(obs_rows // LANES, LANES)
+        for column in (obs_value, obs_precision, obs_row, obs_patch[:, 0])
+    ]
+    recv, late, got = exchange(background, obs_ens.T, lines, capacity)
     for shift in range(1, members):
         ring = [(k, (k + shift) % members) for k in range(members)]
         late[shift] = lax.ppermute(late[shift], "member", ring)
@@ -476,9 +555,8 @@
     if rows % TILE:
         return apply_plain(recv, late, transform, members)
     wide = widen(transform, members)
-    early = recv.shape[1]
-    out = apply_transform([recv], wide, members, channels, 0, math.gcd(early, 2))
-    return apply_transform(late, wide, members, channels, early, 1, out)
+    out = apply_early(recv, wide, members, channels, late[0].shape[1])
+    return apply_late(late, wide, members, out)
 
 
 def solution(mesh):

time: 274 us -> 274 us (level)
  the two profiles are of different devices: /device:TPU:11 before, /device:TPU:0 now
where the time goes in v1:
time: 274 us; the launch traced here: 273 us
  Pallas kernels  245 us (89%)
  starting transfers between devices  13.1 us (5%)
  matrix products  12.4 us (5%)
    pallas_call x1, Pallas kernels, exchange(): pl.pallas_call(functools.partial(exchange_kernel, members, regions, late)...  219 us
    ppermute x3, starting transfers between devices, local(): late[shift] = lax.ppermute(late[shift], 'member', ring)  13.1 us
    dot_general x12, matrix products, batched(): jnp.einsum('bij,bjk->bik', left, right, precision=lax.Precision.HIGHEST)  10.9 us
    pallas_call x1, Pallas kernels, apply_early(): pl.pallas_call(functools.partial(apply_kernel, members), grid=(pl.cdiv(co...  10.1 us
    pallas_call x1, Pallas kernels, band_grams(): pl.pallas_call(functools.partial(gram_kernel, width, lat_rows), grid=(dev...  9.8 us
  transfers between devices with their start and end apart: 3, of which 0 were waited for; matrix products, arithmetic and copies ran while one was open for 5% of the time, Pallas kernels for 8%

profile of v1, /device:TPU:0, one launch (start us, length us, event | category | flops | bytes accessed | tf_op | source)
XLA Modules:
  0.0 273.4 jit_solution(11661697926899059076)
XLA Ops:
  0.0 219.4 %shard_map.64 = (bf16[8,11,16,24,128]{4,3,2,1,0:T(8,128)(2,1)}, bf16[2,2,16,24,128]{4,3,2,1,0:T(8,128)(2,1)}, bf16[2,2,16,24,128]{4,3,2,1,0:T(8,128)(2,1)}, bf16...) custom-call(bf16[16,13,24,1024]{3,2,1,0:T(8,128)(2,1)} %bg_ref.1, ...), custom_call_target="tpu_custom_call" | custom-call | flops 17179869184 | bytes 20447232 | tf_op jit(solution)/shard_map/pallas_call | solution.py:244
  219.4 8.9 %collective-permute-start = (bf16[2,2,16,24,128]{4,3,2,1,0:T(8,128)(2,1)}, bf16[2,2,16,24,128]{4,3,2,1,0:T(8,128)(2,1)S(1)}, u32[]{:S(2)}, u32[]{:S(2)}) collective-permute-start(bf16[2,2,16,24,128]{4,3,2,1,0:T(8,128)(2,1)} %get-tuple-element.17), channel_id=1, source_target_pairs={{0,8},{8,16},{16,24},{24,0},{1,9},{9,17},{17,25},{25,1},{2,10},{10... | collective-permute-start | bytes 1179656 | tf_op jit(solution)/shard_map/ppermute | solution.py:552
  228.2 4.3 %collective-permute-start.1 = (bf16[2,2,16,24,128]{4,3,2,1,0:T(8,128)(2,1)}, bf16[2,2,16,24,128]{4,3,2,1,0:T(8,128)(2,1)S(1)}, u32[]{:S(2)}, u32[]{:S(2)}) collective-permute-start(bf16[2,2,16,24,128]{4,3,2,1,0:T(8,128)(2,1)} %get-tuple-element.18), channel_id=1, source_target_pairs={{0,16},{8,24},{16,0},{24,8},{1,17},{9,25},{17,1},{25,9},{2,18},{10... | collective-permute-start | bytes 1179656 | tf_op jit(solution)/shard_map/ppermute | solution.py:552
  232.5 0.0 collective-permute-start.2
  232.5 1.3 copy-done.1
  233.8 9.8 %shard_map.65 = (f32[1536,64]{1,0:T(8,128)S(1)}, f32[24,64]{1,0:T(8,128)S(1)}) custom-call(bf16[32,72,256]{2,1,0:T(8,128)(2,1)S(1)} %copy-done.1), custom_call_target="tpu_custom_call" | custom-call | flops 6442450944 | bytes 1179648 | tf_op jit(solution)/shard_map/pallas_call | solution.py:321
  243.6 0.3 fusion.5
  243.9 0.1 reduce_sum.14
  243.9 0.1 reduce_sum.18
  244.1 0.9 fusion.3
  245.0 1.0 fusion.9
  246.0 0.8 fusion.6
  246.8 0.9 fusion.2
  247.7 0.9 fusion.14
  248.6 0.9 fusion.13
  249.6 0.9 fusion.1
  250.5 0.9 fusion.15
  251.4 0.0 slice-start
  251.4 0.9 fusion.16
  252.3 0.9 fusion
  253.2 0.0 slice-start.1
  253.3 0.9 fusion.17
  254.2 0.9 convolution_divide_fusion
  255.1 1.5 fusion.18
  256.6 0.3 add_convert_fusion
  257.0 0.0 slice-start.2
  257.0 2.3 shard_map.66.wide_ref
  259.4 10.1 %shard_map.67.refs_4_ = bf16[64,13,48,128]{3,2,1,0:T(8,128)(2,1)} custom-call(bf16[6,512,512]{2,1,0:T(8,128)(2,1)S(1)} %shard_map.66.wide_ref, bf16[8,11,16,24,128]{4,3,2,1,0:T(8,128)(2,1)S(1)} %bitcast.41), custom_call_target="tpu_custom_call" | custom-call | flops 4429185024 | bytes 17301504 | tf_op jit(solution)/shard_map/pallas_call | solution.py:452
  269.5 0.0 collective-permute-done.refs_1_
  269.5 0.0 collective-permute-done.1.refs_2_
  269.5 0.0 collective-permute-done.2.refs_3_
  269.5 3.8 %shard_map.68 = bf16[64,13,48,128]{3,2,1,0:T(8,128)(2,1)} custom-call(bf16[6,512,512]{2,1,0:T(8,128)(2,1)S(1)} %shard_map.66.wide_ref, bf16[2,2,16,24,128]{4,3,2,1,0:T(8,128)(2,1)S(1)} %copy-done, bf16[2,2,16,24,128]{4,3,2,1,0:T(8,128)(2,1)S(1)} %collective-permute-done.refs_1_, ...), custom_call_target="tpu_custom_call", output_to_operand_aliasing={{}: (5, {})} | custom-call | flops 805306368 | bytes 3145728 | tf_op jit(solution)/shard_map/pallas_call | solution.py:496
  (10 shorter events, 0.0 us)
Async XLA Ops:
  219.4 50.1 %collective-permute-start = (bf16[2,2,16,24,128]{4,3,2,1,0:T(8,128)(2,1)}, bf16[2,2,16,24,128]{4,3,2,1,0:T(8,128)(2,1)S(1)}, u32[]{:S(2)}, u32[]{:S(2)}) collective-permute-start(bf16[2,2,16,24,128]{4,3,2,1,0:T(8,128)(2,1)} %get-tuple-element.17), channel_id=1, source_target_pairs={{0,8},{8,16},{16,24},{24,0},{1,9},{9,17},{17,25},{25,1},{2,10},{10... | collective-permute-start | bytes 1179656 | tf_op jit(solution)/shard_map/ppermute | solution.py:552
  228.2 41.3 %collective-permute-start.1 = (bf16[2,2,16,24,128]{4,3,2,1,0:T(8,128)(2,1)}, bf16[2,2,16,24,128]{4,3,2,1,0:T(8,128)(2,1)S(1)}, u32[]{:S(2)}, u32[]{:S(2)}) collective-permute-start(bf16[2,2,16,24,128]{4,3,2,1,0:T(8,128)(2,1)} %get-tuple-element.18), channel_id=1, source_target_pairs={{0,16},{8,24},{16,0},{24,8},{1,17},{9,25},{17,1},{25,9},{2,18},{10... | collective-permute-start | bytes 1179656 | tf_op jit(solution)/shard_map/ppermute | solution.py:552
  232.5 37.0 %collective-permute-start.2 = (bf16[2,2,16,24,128]{4,3,2,1,0:T(8,128)(2,1)}, bf16[2,2,16,24,128]{4,3,2,1,0:T(8,128)(2,1)S(1)}, u32[]{:S(2)}, u32[]{:S(2)}) collective-permute-start(bf16[2,2,16,24,128]{4,3,2,1,0:T(8,128)(2,1)} %get-tuple-element.19), channel_id=1, source_target_pairs={{0,24},{8,0},{16,8},{24,16},{1,25},{9,1},{17,9},{25,17},{2,26},{10... | collective-permute-start | bytes 1179656 | tf_op jit(solution)/shard_map/ppermute | solution.py:552
  232.5 1.3 copy-start.1
  251.4 7.9 %slice-start = ((s8[8650752]{0:T(1024)(128)(4,1)}), s8[4194304]{0:T(1024)(128)(4,1)S(1)}, s32[]{:S(2)}) async-start(s8[8650752]{0:T(1024)(128)(4,1)} %bitcast.40), calls=%async_computation | async-start | bytes 8388608
  253.2 6.1 %slice-start.1 = ((s8[8650752]{0:T(1024)(128)(4,1)}), s8[4194304]{0:T(1024)(128)(4,1)S(1)}, s32[]{:S(2)}) async-start(s8[8650752]{0:T(1024)(128)(4,1)} %bitcast.40), calls=%async_computation.1 | async-start | bytes 8388608
  257.0 2.4 slice-start.2
  259.4 10.1 %copy-start = (bf16[2,2,16,24,128]{4,3,2,1,0:T(8,128)(2,1)S(1)}, bf16[2,2,16,24,128]{4,3,2,1,0:T(8,128)(2,1)}, u32[]{:S(2)}) copy-start(bf16[2,2,16,24,128]{4,3,2,1,0:T(8,128)(2,1)} %get-tuple-element.16.refs_0_) | copy-start | bytes 1179652

commit v2 on v1

--- a/solution.py
+++ b/solution.py
@@ -18,27 +18,81 @@
 MESH = pl.DeviceIdType.MESH
 
 
+def add_gram(got_ref, kind, lat_rows, sum_ref, scaled_ref):
+    sources, cols, capacity = got_ref.shape[1:]
+    width = cols - EXTRAS
+    bands = lat_rows // BAND
+    lower = bands * width // 2
+    group = max(1, math.gcd(sources, 1024 // capacity))
+    sum_ref[...] = jnp.zeros_like(sum_ref)
+
+    def step(i, carry):
+        block = jnp.concatenate(
+            [got_ref[kind, i * group + k].astype(jnp.float32) for k in range(group)], axis=1
+        )
+        ens = block[:width]
+        obs_val, obs_prec, row = (block[width + k : width + k + 1] for k in range(3))
+        mean = jnp.sum(ens, axis=0, keepdims=True) / width
+        pert = (ens - mean).astype(jnp.bfloat16)
+        pert_float = pert.astype(jnp.float32)
+        innovation = obs_val - mean
+        index = lax.broadcasted_iota(jnp.int32, (bands, 1), 0).astype(jnp.float32)
+        distance = (row - (index * BAND + (BAND - 1) / 2.0)) / (lat_rows / 4.0)
+        weight = obs_prec * jnp.exp(-0.5 * distance * distance)
+        for j in range(bands):
+            scaled_ref[j * width : (j + 1) * width, :] = (
+                weight[j : j + 1] * pert_float
+            ).astype(jnp.bfloat16)
+        empty = jnp.zeros_like(pert)
+        over_obs = (((1,), (1,)), ((), ()))
+        sum_ref[:lower] += lax.dot_general(
+            scaled_ref[:lower], jnp.concatenate([pert, empty], axis=0), over_obs,
+            preferred_element_type=jnp.float32,
+        ) + lax.dot_general(
+            scaled_ref[lower:], jnp.concatenate([empty, pert], axis=0), over_obs,
+            preferred_element_type=jnp.float32,
+        )
+        sum_ref[lower:] += lax.dot_general(
+            weight * innovation,
+            jnp.concatenate([pert_float, jnp.zeros_like(pert_float)], axis=0),
+            over_obs,
+            precision=lax.Precision.HIGHEST,
+            preferred_element_type=jnp.float32,
+        )
+        return carry
+
+    lax.fori_loop(0, sources // group, step, 0)
+
+
 def exchange_kernel(
     members, regions, late, bg_ref, ens_ref, value_ref, precision_ref, row_ref, patch_ref, *refs
 ):
     strips = regions // members
+    half = members // 2
     devices = members * regions
-    channels = bg_ref.shape[1]
+    sources = half * regions
+    local_members, channels, rows, _ = bg_ref.shape
     recv_ref, own_ref = refs[:2]
     lift_refs = refs[2 : 1 + members]
-    got_ref = refs[1 + members]
+    near_ref, far_ref = refs[1 + members : 3 + members]
     (
-        held_ref, packed_ref, pair_ref, whole_ref, extra_ref, rank_ref, obs_ref,
+        held_ref, packed_ref, pair_ref, whole_ref, extra_ref, rank_ref, obs_ref, got_ref,
+        sum_ref, scaled_ref,
         local_sem, spread_send, spread_recv, lift_send, lift_recv, out_sem,
-        in_sem, obs_sem,
-    ) = refs[2 + members :]
+        in_sem, obs_sem, gram_sem,
+    ) = refs[3 + members :]
     width, obs_rows = ens_ref.shape
     capacity = obs_ref.shape[2]
     m, r = lax.axis_index("member"), lax.axis_index("region")
-    me = m * regions + r
     home, seat = lax.div(r, strips), lax.rem(r, strips)
+    side, level = lax.div(m, half), lax.rem(m, half)
     first_stage = members * strips
     order = list(range(late, channels)) + list(range(late))
+    early = order[: channels - late]
+    pieces = math.gcd(local_members, 4)
+    cut = local_members // pieces
+    units = [(order[0], k * cut, (k + 1) * cut) for k in range(pieces)]
+    units += [(c, 0, local_members) for c in order[1:]]
 
     copies_in = [
         pltpu.make_async_copy(ens_ref, packed_ref.at[0:width], in_sem.at[0]),
@@ -47,81 +101,101 @@
         pltpu.make_async_copy(row_ref, whole_ref.at[0], in_sem.at[3]),
         pltpu.make_async_copy(patch_ref, whole_ref.at[1], in_sem.at[4]),
     ]
+    barrier = pltpu.get_barrier_semaphore()
+    for d in range(1, members):
+        pl.semaphore_signal(
+            barrier, inc=1, device_id={"member": lax.rem(m + d, members)}, device_id_type=MESH
+        )
+
+    def greet(d, carry):
+        pl.semaphore_signal(
+            barrier, inc=1, device_id={"region": lax.rem(r + d, regions)}, device_id_type=MESH
+        )
+        return carry
+
+    lax.fori_loop(1, regions, greet, 0)
     for copy in copies_in:
         copy.start()
-    barrier = pltpu.get_barrier_semaphore()
-
-    def at_device(other):
-        return {"member": lax.div(other, regions), "region": lax.rem(other, regions)}
-
-    def greet(d, carry):
-        other = lax.rem(me + d, devices)
-        pl.semaphore_signal(
-            barrier, inc=1, device_id=at_device(other), device_id_type=MESH
-        )
-        return carry
-
-    lax.fori_loop(1, devices, greet, 0)
-    pl.semaphore_wait(barrier, devices - 1)
-
     slot = jnp.where(home == m, seat, first_stage + r)
     groups = [0] + sorted(range(1, members), key=lambda g: (abs(2 * g - members), g))
 
-    def block(c, b):
-        return bg_ref.at[:, c, :, pl.ds(pl.multiple_of(b * LANES, LANES), LANES)]
-
-    def spread(c, b):
+    def block(u, b):
+        c, low, high = units[u]
+        return bg_ref.at[low:high, c, :, pl.ds(pl.multiple_of(b * LANES, LANES), LANES)]
+
+    def place_of(u, where):
+        c, low, high = units[u]
+        return held_ref.at[where, c, low:high]
+
+    def own_copy(u):
+        return pltpu.make_async_copy(block(u, r), place_of(u, slot), local_sem.at[u])
+
+    def spread(u, b):
         pltpu.make_async_remote_copy(
-            block(c, b), held_ref.at[slot, c], spread_send.at[c], spread_recv.at[c, home],
+            block(u, b), place_of(u, slot), spread_send.at[units[u][0]],
+            spread_recv.at[u, home],
             device_id={"region": b}, device_id_type=MESH,
         ).start()
 
-    for c in order:
-        pltpu.make_async_copy(block(c, r), held_ref.at[slot, c], local_sem.at[c]).start()
+    def issue(u):
+        if u >= len(units):
+            return
+        if u:
+            own_copy(u).start()
         for j in range(1, strips):
-            spread(c, home * strips + lax.rem(seat + j, strips))
+            spread(u, home * strips + lax.rem(seat + j, strips))
         for g in groups[1:]:
 
-            def spread_group(j, carry, c=c, g=g):
-                spread(c, lax.rem(home + g, members) * strips + j)
+            def spread_group(j, carry, g=g):
+                spread(u, lax.rem(home + g, members) * strips + j)
                 return carry
 
             lax.fori_loop(0, strips, spread_group, 0)
 
+    own_copy(0).start()
+    pl.semaphore_wait(barrier, regions + members - 2)
+
     lifted = (members - 1) * strips
 
-    def arrive(c, g):
+    def arrive(u, g):
+        c, low, high = units[u]
         a = lax.rem(home + g, members)
         if g == 0:
-            pltpu.make_async_copy(held_ref.at[0, c], held_ref.at[0, c], local_sem.at[c]).wait()
+            own_copy(u).wait()
         if g or strips > 1:
-            some = held_ref.at[0 : strips if g else strips - 1, c]
-            pltpu.make_async_copy(some, some, spread_recv.at[c, a]).wait()
+            some = held_ref.at[0 : strips if g else strips - 1, c, low:high]
+            pltpu.make_async_copy(some, some, spread_recv.at[u, a]).wait()
         return a
 
-    def forward(c, g):
-        a = arrive(c, g)
+    def forward(u, g):
+        c = units[u][0]
+        a = arrive(u, g)
         s = lax.rem(a - m + members, members)
 
         @pl.when(a != m)
         def _():
             for j in range(strips):
                 pltpu.make_async_remote_copy(
-                    held_ref.at[first_stage + a * strips + j, c],
-                    held_ref.at[s * strips + j, c],
+                    place_of(u, first_stage + a * strips + j),
+                    place_of(u, s * strips + j),
                     lift_send.at[c], lift_recv.at[c],
                     device_id={"member": a}, device_id_type=MESH,
                 ).start()
 
-    early = order[: channels - late]
-    ahead = early[: min(3, len(early))]
-    for c in ahead:
-        forward(c, 0)
-
-    def forward_rest(c):
+    window = pieces + 2
+    for u in range(pieces):
+        issue(u)
+        forward(u, 0)
+    for u in range(pieces, window):
+        issue(u)
+    for g in groups[1:]:
+        for u in range(pieces):
+            forward(u, g)
+
+    def forward_all(u):
         for g in groups:
-            if g or c not in ahead:
-                forward(c, g)
+            forward(u, g)
+        issue(u + 2)
 
     for copy in copies_in:
         copy.wait()
@@ -165,24 +239,63 @@
         obs_ref[d] = total.astype(jnp.bfloat16)
         return carry
 
-    stages = min(4, len(early) - 1)
+    rest = list(range(pieces, pieces + len(early) - 1))
+    stages = min(4, len(rest) - 1)
     for k in range(stages):
-        forward_rest(early[k])
         lax.fori_loop(devices * k // stages, devices * (k + 1) // stages, place, 0)
-    forward_rest(early[stages])
-
-    def send_obs(d, carry):
-        other = lax.rem(me + d, devices)
-        pltpu.make_async_remote_copy(
-            obs_ref.at[other], got_ref.at[me], obs_sem.at[0], obs_sem.at[1],
-            device_id=at_device(other), device_id_type=MESH,
-        ).start()
+        forward_all(rest[k])
+
+    def early_copy(c):
+        return pltpu.make_async_copy(
+            held_ref.at[0:first_stage, c], recv_ref.at[:, c - late], out_sem.at[c, 0]
+        )
+
+    def lift_done(c):
+        lift_all = held_ref.at[0:lifted, c]
+        pltpu.make_async_copy(lift_all, lift_all, lift_recv.at[c]).wait()
+        early_copy(c).start()
+
+    lift_done(early[0])
+    mine = level * regions + r
+
+    def send_obs(i, carry):
+        to = lax.rem(mine + i, sources)
+        where = {
+            "member": side * half + lax.div(to, regions),
+            "region": lax.rem(to, regions),
+        }
+        for kind in range(2):
+            half_of = lax.rem(side + kind, 2)
+            pltpu.make_async_remote_copy(
+                obs_ref.at[half_of * sources + to], got_ref.at[kind, mine],
+                obs_sem.at[kind], obs_sem.at[2 + kind],
+                device_id=where, device_id_type=MESH,
+            ).start()
         return carry
 
-    lax.fori_loop(1, devices, send_obs, 0)
-    pltpu.make_async_copy(obs_ref.at[me], got_ref.at[me], obs_sem.at[2]).start()
-    for c in early[stages + 1 :]:
-        forward_rest(c)
+    lax.fori_loop(1, sources, send_obs, 0)
+    for kind in range(2):
+        got_ref[kind, mine] = obs_ref[lax.rem(side + kind, 2) * sources + mine]
+    for u in rest[stages:]:
+        forward_all(u)
+    for u in range(rest[-1] + 3, len(units)):
+        issue(u)
+
+    def obs_all(kind, sem):
+        some = got_ref.at[kind, 0 : sources - 1]
+        pltpu.make_async_copy(some, some, obs_sem.at[sem]).wait()
+
+    lat_rows = strips * rows
+    for kind in (1, 0):
+        obs_all(kind, 2 + kind)
+        add_gram(got_ref, kind, lat_rows, sum_ref.at[kind], scaled_ref)
+    far = pltpu.make_async_remote_copy(
+        sum_ref.at[1], far_ref, gram_sem.at[0], gram_sem.at[1],
+        device_id={"member": lax.rem(m + half, members)}, device_id_type=MESH,
+    )
+    far.start()
+    near = pltpu.make_async_copy(sum_ref.at[0], near_ref, gram_sem.at[2])
+    near.start()
 
     def late_copies(c):
         copies = [
@@ -199,28 +312,18 @@
             )
         return copies
 
-    for c in range(late):
+    for u in range(len(units) - late, len(units)):
         for g in groups:
-            arrive(c, g)
-        for copy in late_copies(c):
+            arrive(u, g)
+        for copy in late_copies(units[u][0]):
             copy.start()
-
-    def early_copy(c):
-        return pltpu.make_async_copy(
-            held_ref.at[0:first_stage, c], recv_ref.at[:, c - late], out_sem.at[c, 0]
-        )
-
-    for c in early:
-        lift_all = held_ref.at[0:lifted, c]
-        pltpu.make_async_copy(lift_all, lift_all, lift_recv.at[c]).wait()
-        early_copy(c).start()
+    for c in early[1:]:
+        lift_done(c)
     for c in range(channels):
         spread_all = held_ref.at[0 : regions - 1, c]
         pltpu.make_async_copy(spread_all, spread_all, spread_send.at[c]).wait()
-    obs_all = got_ref.at[0 : devices - 1]
-    pltpu.make_async_copy(obs_all, obs_all, obs_sem.at[0]).wait()
-    pltpu.make_async_copy(obs_all, obs_all, obs_sem.at[1]).wait()
-    pltpu.make_async_copy(obs_ref.at[0], got_ref.at[0], obs_sem.at[2]).wait()
+    for kind in range(2):
+        obs_all(kind, kind)
     for c in range(late):
         for copy in late_copies(c):
             copy.wait()
@@ -228,30 +331,37 @@
         lift_all = held_ref.at[0:lifted, c]
         pltpu.make_async_copy(lift_all, lift_all, lift_send.at[c]).wait()
         early_copy(c).wait()
+    near.wait()
+    far.wait()
 
 
 def exchange(background, ens_cols, lines, capacity):
     members, regions = lax.axis_size("member"), lax.axis_size("region")
     strips = regions // members
     devices = members * regions
+    sources = devices // 2
     local_members, channels, rows, _ = background.shape
     width, obs_rows = ens_cols.shape
     obs_lines = obs_rows // LANES
     late = min(LATE, channels - 2)
+    bands = strips * rows // BAND
+    units = channels - 1 + math.gcd(local_members, 4)
+    group = max(1, math.gcd(sources, 1024 // capacity))
     dma = pltpu.SemaphoreType.DMA
     kind = background.dtype
     part = jax.ShapeDtypeStruct((strips, late, local_members, rows, LANES), kind)
+    total = (bands * width // 2 + bands, 2 * width)
     out = pl.pallas_call(
         functools.partial(exchange_kernel, members, regions, late),
         in_specs=[pl.BlockSpec(memory_space=pl.ANY)] * 6,
-        out_specs=[pl.BlockSpec(memory_space=pl.ANY)] * (members + 2),
+        out_specs=[pl.BlockSpec(memory_space=pl.ANY)] * (members + 3),
         out_shape=[
             jax.ShapeDtypeStruct(
                 (members * strips, channels - late, local_members, rows, LANES), kind
             )
         ]
         + [part] * members
-        + [jax.ShapeDtypeStruct((devices, width + EXTRAS, capacity), jnp.bfloat16)],
+        + [jax.ShapeDtypeStruct(total, jnp.float32)] * 2,
         scratch_shapes=[
             pltpu.VMEM(
                 (members * strips + regions, channels, local_members, rows, LANES), kind
@@ -262,11 +372,13 @@
             pltpu.VMEM((EXTRAS, obs_rows), jnp.float32),
             pltpu.VMEM((1, obs_rows), jnp.float32),
             pltpu.VMEM((devices, width + EXTRAS, capacity), jnp.bfloat16),
+            pltpu.VMEM((2, sources, width + EXTRAS, capacity), jnp.bfloat16),
+            pltpu.VMEM((2,) + total, jnp.float32),
+            pltpu.VMEM((bands * width, group * capacity), jnp.bfloat16),
         ]
+        + [dma((units,)), dma((channels,)), dma((units, members))]
         + [dma((channels,))] * 2
-        + [dma((channels, members))]
-        + [dma((channels,))] * 2
-        + [dma((channels, members)), dma((5,)), dma((3,))],
+        + [dma((channels, members)), dma((5,)), dma((4,)), dma((3,))],
         compiler_params=pltpu.CompilerParams(
             collective_id=0, has_side_effects=True, vmem_limit_bytes=60 << 20
         ),
@@ -274,71 +386,20 @@
             flops=1 << 34, bytes_accessed=4 * background.size, transcendentals=0
         ),
     )(background, ens_cols, *lines)
-    return out[0], list(out[1 : 1 + members]), out[1 + members]
-
-
-def gram_kernel(width, lat_rows, got_ref, gram_ref, proj_ref, scaled_ref):
-    bands = lat_rows // BAND
-
-    @pl.when(pl.program_id(0) == 0)
-    def _():
-        gram_ref[...] = jnp.zeros_like(gram_ref)
-        proj_ref[...] = jnp.zeros_like(proj_ref)
-
-    cols = jnp.concatenate(
-        [got_ref[k].astype(jnp.float32) for k in range(got_ref.shape[0])], axis=1
+    return out[0], list(out[1 : 1 + members]), out[1 + members], out[2 + members]
+
+
+def total_grams(near, far, bands):
+    width = near.shape[1] // 2
+    total = near + far
+    lower = bands * width // 2
+    gram = jnp.concatenate(
+        [
+            total[:lower, :width].reshape(bands // 2, width, width),
+            total[:lower, width:].reshape(bands // 2, width, width),
+        ]
     )
-    ens = cols[:width]
-    obs_val, obs_prec, row = (cols[width + k : width + k + 1] for k in range(3))
-    mean = jnp.sum(ens, axis=0, keepdims=True) / width
-    pert = (ens - mean).astype(jnp.bfloat16)
-    pert_float = pert.astype(jnp.float32)
-    innovation = obs_val - mean
-    index = lax.broadcasted_iota(jnp.int32, (bands, 1), 0).astype(jnp.float32)
-    distance = (row - (index * BAND + (BAND - 1) / 2.0)) / (lat_rows / 4.0)
-    weight = obs_prec * jnp.exp(-0.5 * distance * distance)
-    for j in range(bands):
-        scaled_ref[j * width : (j + 1) * width, :] = (weight[j : j + 1] * pert_float).astype(
-            jnp.bfloat16
-        )
-    over_obs = (((1,), (1,)), ((), ()))
-    gram_ref[...] += lax.dot_general(
-        scaled_ref[...], pert, over_obs, preferred_element_type=jnp.float32
-    )
-    proj_ref[...] += lax.dot_general(
-        weight * innovation,
-        pert_float,
-        over_obs,
-        precision=lax.Precision.HIGHEST,
-        preferred_element_type=jnp.float32,
-    )
-
-
-def band_grams(got, width, lat_rows):
-    devices, cols, capacity = got.shape
-    bands = lat_rows // BAND
-    group = max(1, math.gcd(devices, 1024 // capacity))
-    gram, projected = pl.pallas_call(
-        functools.partial(gram_kernel, width, lat_rows),
-        grid=(devices // group,),
-        in_specs=[pl.BlockSpec((group, cols, capacity), lambda i: (i, 0, 0))],
-        out_specs=[
-            pl.BlockSpec((bands * width, width), lambda i: (0, 0)),
-            pl.BlockSpec((bands, width), lambda i: (0, 0)),
-        ],
-        out_shape=[
-            jax.ShapeDtypeStruct((bands * width, width), jnp.float32),
-            jax.ShapeDtypeStruct((bands, width), jnp.float32),
-        ],
-        scratch_shapes=[pltpu.VMEM((bands * width, group * capacity), jnp.bfloat16)],
-        compiler_params=pltpu.CompilerParams(vmem_limit_bytes=24 << 20),
-        cost_estimate=pl.CostEstimate(
-            flops=8 * devices * capacity * bands * width * width,
-            bytes_accessed=2 * devices * capacity * cols,
-            transcendentals=devices * capacity * bands,
-        ),
-    )(got)
-    return gram.reshape(bands, width, width), projected
+    return gram, total[lower:, :width]
 
 
 def batched(left, right):
@@ -351,8 +412,10 @@
     system = (members - 1.0) * identity + gram_band
     norm_f = jnp.sqrt(jnp.sum(system * system, axis=(1, 2)))
     root_iter = system / norm_f[:, None, None]
-    inv_root = jnp.broadcast_to(identity, system.shape)
-    for _ in range(NS_ITERS):
+    middle = 1.5 * identity - 0.5 * root_iter
+    root_iter = batched(root_iter, middle)
+    inv_root = middle
+    for _ in range(1, NS_ITERS):
         middle = 1.5 * identity - 0.5 * batched(inv_root, root_iter)
         root_iter = batched(root_iter, middle)
         inv_root = batched(middle, inv_root)
@@ -546,12 +609,11 @@
         column.reshape(obs_rows // LANES, LANES)
         for column in (obs_value, obs_precision, obs_row, obs_patch[:, 0])
     ]
-    recv, late, got = exchange(background, obs_ens.T, lines, capacity)
+    recv, late, near, far = exchange(background, obs_ens.T, lines, capacity)
     for shift in range(1, members):
         ring = [(k, (k + shift) % members) for k in range(members)]
         late[shift] = lax.ppermute(late[shift], "member", ring)
-    grams = band_grams(got, width, lat_rows)
-    transform = band_transforms(grams, width)
+    transform = band_transforms(total_grams(near, far, lat_rows // BAND), width)
     if rows % TILE:
         return apply_plain(recv, late, transform, members)
     wide = widen(transform, members)

time: 274 us -> 256 us (0.934)
  the two profiles are of different devices: /device:TPU:0 before, /device:TPU:12 now
where the time goes in v2:
time: 256 us
  Pallas kernels  225 us (88%)
  matrix products  10.9 us (4%)
  starting transfers between devices  8.69 us (3%)
  waiting for transfers between devices  8.2 us (3%)
    pallas_call x1, Pallas kernels, exchange(): pl.pallas_call(functools.partial(exchange_kernel, members, regions, late)...  209 us
    pallas_call x1, Pallas kernels, apply_early(): pl.pallas_call(functools.partial(apply_kernel, members), grid=(pl.cdiv(co...  10.1 us
    dot_general x10, matrix products, batched(): jnp.einsum('bij,bjk->bik', left, right, precision=lax.Precision.HIGHEST)  9.62 us
    ppermute x3, starting transfers between devices, local(): late[shift] = lax.ppermute(late[shift], 'member', ring)  8.69 us
    ppermute x3, waiting for transfers between devices, local(): late[shift] = lax.ppermute(late[shift], 'member', ring)  8.2 us
  transfers between devices with their start and end apart: 3, of which 2 were waited for; matrix products, arithmetic and copies ran while one was open for 5% of the time, Pallas kernels for 5%

profile of v2, /device:TPU:12, one launch (start us, length us, event | category | flops | bytes accessed | tf_op | source)
XLA Modules:
  0.0 255.7 jit_solution(13845692574060263800)
XLA Ops:
  0.0 209.0 %shard_map.64 = (bf16[8,11,16,24,128]{4,3,2,1,0:T(8,128)(2,1)}, bf16[2,2,16,24,128]{4,3,2,1,0:T(8,128)(2,1)}, bf16[2,2,16,24,128]{4,3,2,1,0:T(8,128)(2,1)}, bf16...) custom-call(bf16[16,13,24,1024]{3,2,1,0:T(8,128)(2,1)} %bg_ref.1, ...), custom_call_target="tpu_custom_call" | custom-call | flops 17179869184 | bytes 20447232 | tf_op jit(solution)/shard_map/pallas_call | solution.py:354
  209.0 4.3 %collective-permute-start = (bf16[2,2,16,24,128]{4,3,2,1,0:T(8,128)(2,1)}, bf16[2,2,16,24,128]{4,3,2,1,0:T(8,128)(2,1)S(1)}, u32[]{:S(2)}, u32[]{:S(2)}) collective-permute-start(bf16[2,2,16,24,128]{4,3,2,1,0:T(8,128)(2,1)} %get-tuple-element.15), channel_id=1, source_target_pairs={{0,8},{8,16},{16,24},{24,0},{1,9},{9,17},{17,25},{25,1},{2,10},{10... | collective-permute-start | bytes 1179656 | tf_op jit(solution)/shard_map/ppermute | solution.py:615
  213.3 4.4 %collective-permute-start.1 = (bf16[2,2,16,24,128]{4,3,2,1,0:T(8,128)(2,1)}, bf16[2,2,16,24,128]{4,3,2,1,0:T(8,128)(2,1)S(1)}, u32[]{:S(2)}, u32[]{:S(2)}) collective-permute-start(bf16[2,2,16,24,128]{4,3,2,1,0:T(8,128)(2,1)} %get-tuple-element.16), channel_id=1, source_target_pairs={{0,16},{8,24},{16,0},{24,8},{1,17},{9,25},{17,1},{25,9},{2,18},{10... | collective-permute-start | bytes 1179656 | tf_op jit(solution)/shard_map/ppermute | solution.py:615
  217.7 0.0 collective-permute-start.2
  217.7 1.2 add.20
  218.9 0.2 fusion.20
  219.1 0.3 multiply_reduce_fusion
  219.4 1.1 fusion.4
  220.5 1.1 fusion.2
  221.6 1.0 fusion.3
  222.6 0.9 fusion.21
  223.6 0.9 fusion.1
  224.5 0.9 fusion.22
  225.4 0.0 slice-start
  225.4 0.9 fusion.23
  226.3 0.9 fusion
  227.2 0.0 slice-start.1
  227.3 0.9 fusion.24
  228.2 0.9 convolution_divide_fusion
  229.1 1.3 fusion.25
  230.4 0.3 add_convert_fusion
  230.7 0.0 slice-start.2
  230.8 2.6 %shard_map.65.wide_ref = bf16[6,512,512]{2,1,0:T(8,128)(2,1)S(1)} custom-call(bf16[24,4,16,64]{3,2,1,0:T(8,128)(2,1)S(1)} %bitcast.33), custom_call_target="tpu_custom_call" | custom-call | flops 2147483648 | bytes 2097152 | tf_op jit(solution)/shard_map/pallas_call | solution.py:457
  233.3 0.0 slice-done
  233.3 0.0 slice-done.1
  233.4 0.0 slice-done.2
  233.4 10.1 %shard_map.66.refs_4_ = bf16[64,13,48,128]{3,2,1,0:T(8,128)(2,1)} custom-call(bf16[6,512,512]{2,1,0:T(8,128)(2,1)S(1)} %shard_map.65.wide_ref, bf16[8,11,16,24,128]{4,3,2,1,0:T(8,128)(2,1)S(1)} %bitcast.32), custom_call_target="tpu_custom_call" | custom-call | flops 4429185024 | bytes 17301504 | tf_op jit(solution)/shard_map/pallas_call | solution.py:515
  243.5 0.0 collective-permute-done.refs_1_
  243.5 4.5 %collective-permute-done.1.refs_2_ = bf16[2,2,16,24,128]{4,3,2,1,0:T(8,128)(2,1)S(1)} collective-permute-done((bf16[2,2,16,24,128]{4,3,2,1,0:T(8,128)(2,1)}, bf16[2,2,16,24,128]{4,3,2,1,0:T(8,128)(2,1)S(1)}, u32[]{:S(2)}, u32[]{:S(2)}) %collective-permute-start.1) | collective-permute-done | bytes 393248 | tf_op jit(solution)/shard_map/ppermute | solution.py:615
  248.0 3.7 %collective-permute-done.2.refs_3_ = bf16[2,2,16,24,128]{4,3,2,1,0:T(8,128)(2,1)S(1)} collective-permute-done((bf16[2,2,16,24,128]{4,3,2,1,0:T(8,128)(2,1)}, bf16[2,2,16,24,128]{4,3,2,1,0:T(8,128)(2,1)S(1)}, u32[]{:S(2)}, u32[]{:S(2)}) %collective-permute-start.2) | collective-permute-done | bytes 393248 | tf_op jit(solution)/shard_map/ppermute | solution.py:615
  251.7 0.0 copy-done
  251.7 3.8 %shard_map.67 = bf16[64,13,48,128]{3,2,1,0:T(8,128)(2,1)} custom-call(bf16[6,512,512]{2,1,0:T(8,128)(2,1)S(1)} %shard_map.65.wide_ref, bf16[2,2,16,24,128]{4,3,2,1,0:T(8,128)(2,1)S(1)} %copy-done, bf16[2,2,16,24,128]{4,3,2,1,0:T(8,128)(2,1)S(1)} %collective-permute-done.refs_1_, ...), custom_call_target="tpu_custom_call", output_to_operand_aliasing={{}: (5, {})} | custom-call | flops 805306368 | bytes 3145728 | tf_op jit(solution)/shard_map/pallas_call | solution.py:559
  (5 shorter events, 0.0 us)
Async XLA Ops:
  209.0 34.5 %collective-permute-start = (bf16[2,2,16,24,128]{4,3,2,1,0:T(8,128)(2,1)}, bf16[2,2,16,24,128]{4,3,2,1,0:T(8,128)(2,1)S(1)}, u32[]{:S(2)}, u32[]{:S(2)}) collective-permute-start(bf16[2,2,16,24,128]{4,3,2,1,0:T(8,128)(2,1)} %get-tuple-element.15), channel_id=1, source_target_pairs={{0,8},{8,16},{16,24},{24,0},{1,9},{9,17},{17,25},{25,1},{2,10},{10... | collective-permute-start | bytes 1179656 | tf_op jit(solution)/shard_map/ppermute | solution.py:615
  213.3 34.7 %collective-permute-start.1 = (bf16[2,2,16,24,128]{4,3,2,1,0:T(8,128)(2,1)}, bf16[2,2,16,24,128]{4,3,2,1,0:T(8,128)(2,1)S(1)}, u32[]{:S(2)}, u32[]{:S(2)}) collective-permute-start(bf16[2,2,16,24,128]{4,3,2,1,0:T(8,128)(2,1)} %get-tuple-element.16), channel_id=1, source_target_pairs={{0,16},{8,24},{16,0},{24,8},{1,17},{9,25},{17,1},{25,9},{2,18},{10... | collective-permute-start | bytes 1179656 | tf_op jit(solution)/shard_map/ppermute | solution.py:615
  217.7 34.0 %collective-permute-start.2 = (bf16[2,2,16,24,128]{4,3,2,1,0:T(8,128)(2,1)}, bf16[2,2,16,24,128]{4,3,2,1,0:T(8,128)(2,1)S(1)}, u32[]{:S(2)}, u32[]{:S(2)}) collective-permute-start(bf16[2,2,16,24,128]{4,3,2,1,0:T(8,128)(2,1)} %get-tuple-element.17), channel_id=1, source_target_pairs={{0,24},{8,0},{16,8},{24,16},{1,25},{9,1},{17,9},{25,17},{2,26},{10... | collective-permute-start | bytes 1179656 | tf_op jit(solution)/shard_map/ppermute | solution.py:615
  225.4 7.9 %slice-start = ((s8[8650752]{0:T(1024)(128)(4,1)}), s8[4194304]{0:T(1024)(128)(4,1)S(1)}, s32[]{:S(2)}) async-start(s8[8650752]{0:T(1024)(128)(4,1)} %bitcast.31), calls=%async_computation | async-start | bytes 8388608
  227.2 6.1 %slice-start.1 = ((s8[8650752]{0:T(1024)(128)(4,1)}), s8[4194304]{0:T(1024)(128)(4,1)S(1)}, s32[]{:S(2)}) async-start(s8[8650752]{0:T(1024)(128)(4,1)} %bitcast.31), calls=%async_computation.1 | async-start | bytes 8388608
  230.7 2.6 %slice-start.2 = ((s8[8650752]{0:T(1024)(128)(4,1)}), s8[262144]{0:T(1024)(128)(4,1)S(1)}, s32[]{:S(2)}) async-start(s8[8650752]{0:T(1024)(128)(4,1)} %bitcast.31), calls=%async_computation.2 | async-start | bytes 524288
  233.4 18.3 %copy-start = (bf16[2,2,16,24,128]{4,3,2,1,0:T(8,128)(2,1)S(1)}, bf16[2,2,16,24,128]{4,3,2,1,0:T(8,128)(2,1)}, u32[]{:S(2)}) copy-start(bf16[2,2,16,24,128]{4,3,2,1,0:T(8,128)(2,1)} %get-tuple-element.14.refs_0_) | copy-start | bytes 1179652

commit v3 on v2

--- a/solution.py
+++ b/solution.py
@@ -13,7 +13,7 @@
 NS_ITERS = 4
 TILE = 8
 LANES = 128
-LATE = 2
+LATE = 3
 EXTRAS = 8
 MESH = pl.DeviceIdType.MESH
 
@@ -25,6 +25,7 @@
     lower = bands * width // 2
     group = max(1, math.gcd(sources, 1024 // capacity))
     sum_ref[...] = jnp.zeros_like(sum_ref)
+    last = lower + bands
 
     def step(i, carry):
         block = jnp.concatenate(
@@ -52,7 +53,7 @@
             scaled_ref[lower:], jnp.concatenate([empty, pert], axis=0), over_obs,
             preferred_element_type=jnp.float32,
         )
-        sum_ref[lower:] += lax.dot_general(
+        sum_ref[lower:last] += lax.dot_general(
             weight * innovation,
             jnp.concatenate([pert_float, jnp.zeros_like(pert_float)], axis=0),
             over_obs,
@@ -62,6 +63,21 @@
         return carry
 
     lax.fori_loop(0, sources // group, step, 0)
+
+
+def split_gram(sum_ref, sent_ref, bands):
+    width = sum_ref.shape[1] // 2
+    lower = bands * width // 2
+    last = lower + bands
+    gram = sum_ref[:lower]
+    sent_ref[...] = gram.astype(jnp.bfloat16)
+    diagonal = (
+        lax.broadcasted_iota(jnp.int32, (width, 2 * width), 0)
+        == lax.broadcasted_iota(jnp.int32, (width, 2 * width), 1) % width
+    )
+    for j in range(bands // 2):
+        one = jnp.where(diagonal, gram[j * width : (j + 1) * width], 0.0)
+        sum_ref[last + j : last + j + 1] = jnp.sum(one, axis=0, keepdims=True)
 
 
 def exchange_kernel(
@@ -74,20 +90,21 @@
     local_members, channels, rows, _ = bg_ref.shape
     recv_ref, own_ref = refs[:2]
     lift_refs = refs[2 : 1 + members]
-    near_ref, far_ref = refs[1 + members : 3 + members]
+    near_ref, far_ref, edge_ref = refs[1 + members : 4 + members]
     (
         held_ref, packed_ref, pair_ref, whole_ref, extra_ref, rank_ref, obs_ref, got_ref,
-        sum_ref, scaled_ref,
+        sum_ref, sent_ref, scaled_ref,
         local_sem, spread_send, spread_recv, lift_send, lift_recv, out_sem,
         in_sem, obs_sem, gram_sem,
-    ) = refs[3 + members :]
+    ) = refs[4 + members :]
     width, obs_rows = ens_ref.shape
     capacity = obs_ref.shape[2]
     m, r = lax.axis_index("member"), lax.axis_index("region")
     home, seat = lax.div(r, strips), lax.rem(r, strips)
     side, level = lax.div(m, half), lax.rem(m, half)
     first_stage = members * strips
-    order = list(range(late, channels)) + list(range(late))
+    order = list(range(channels))
+    first_late = channels - late
     early = order[: channels - late]
     pieces = math.gcd(local_members, 4)
     cut = local_members // pieces
@@ -247,7 +264,7 @@
 
     def early_copy(c):
         return pltpu.make_async_copy(
-            held_ref.at[0:first_stage, c], recv_ref.at[:, c - late], out_sem.at[c, 0]
+            held_ref.at[0:first_stage, c], recv_ref.at[:, c], out_sem.at[c, 0]
         )
 
     def lift_done(c):
@@ -289,24 +306,35 @@
     for kind in (1, 0):
         obs_all(kind, 2 + kind)
         add_gram(got_ref, kind, lat_rows, sum_ref.at[kind], scaled_ref)
-    far = pltpu.make_async_remote_copy(
-        sum_ref.at[1], far_ref, gram_sem.at[0], gram_sem.at[1],
-        device_id={"member": lax.rem(m + half, members)}, device_id_type=MESH,
-    )
-    far.start()
-    near = pltpu.make_async_copy(sum_ref.at[0], near_ref, gram_sem.at[2])
+        if kind:
+            split_gram(sum_ref.at[1], sent_ref, lat_rows // BAND)
+    lower = sent_ref.shape[0]
+    across = {"member": lax.rem(m + half, members)}
+    far = [
+        pltpu.make_async_remote_copy(
+            sent_ref, far_ref, gram_sem.at[0], gram_sem.at[1],
+            device_id=across, device_id_type=MESH,
+        ),
+        pltpu.make_async_remote_copy(
+            sum_ref.at[1, lower:], edge_ref, gram_sem.at[2], gram_sem.at[3],
+            device_id=across, device_id_type=MESH,
+        ),
+    ]
+    for copy in far:
+        copy.start()
+    near = pltpu.make_async_copy(sum_ref.at[0], near_ref, gram_sem.at[4])
     near.start()
 
     def late_copies(c):
         copies = [
-            pltpu.make_async_copy(held_ref.at[0:strips, c], own_ref.at[:, c], out_sem.at[c, 0])
+            pltpu.make_async_copy(held_ref.at[0:strips, c], own_ref.at[:, c - first_late], out_sem.at[c, 0])
         ]
         for s in range(1, members):
             a = lax.rem(m + s, members)
             copies.append(
                 pltpu.make_async_copy(
                     held_ref.at[pl.ds(first_stage + a * strips, strips), c],
-                    lift_refs[s - 1].at[:, c],
+                    lift_refs[s - 1].at[:, c - first_late],
                     out_sem.at[c, s],
                 )
             )
@@ -324,7 +352,7 @@
         pltpu.make_async_copy(spread_all, spread_all, spread_send.at[c]).wait()
     for kind in range(2):
         obs_all(kind, kind)
-    for c in range(late):
+    for c in order[channels - late :]:
         for copy in late_copies(c):
             copy.wait()
     for c in early:
@@ -332,7 +360,8 @@
         pltpu.make_async_copy(lift_all, lift_all, lift_send.at[c]).wait()
         early_copy(c).wait()
     near.wait()
-    far.wait()
+    for copy in far:
+        copy.wait()
 
 
 def exchange(background, ens_cols, lines, capacity):
@@ -350,18 +379,24 @@
     dma = pltpu.SemaphoreType.DMA
     kind = background.dtype
     part = jax.ShapeDtypeStruct((strips, late, local_members, rows, LANES), kind)
-    total = (bands * width // 2 + bands, 2 * width)
+    lower = bands * width // 2
+    edge = (3 * bands // 2 + 7) // 8 * 8
+    total = (lower + edge, 2 * width)
     out = pl.pallas_call(
         functools.partial(exchange_kernel, members, regions, late),
         in_specs=[pl.BlockSpec(memory_space=pl.ANY)] * 6,
-        out_specs=[pl.BlockSpec(memory_space=pl.ANY)] * (members + 3),
+        out_specs=[pl.BlockSpec(memory_space=pl.ANY)] * (members + 4),
         out_shape=[
             jax.ShapeDtypeStruct(
                 (members * strips, channels - late, local_members, rows, LANES), kind
             )
         ]
         + [part] * members
-        + [jax.ShapeDtypeStruct(total, jnp.float32)] * 2,
+        + [
+            jax.ShapeDtypeStruct(total, jnp.float32),
+            jax.ShapeDtypeStruct((lower, 2 * width), jnp.bfloat16),
+            jax.ShapeDtypeStruct((edge, 2 * width), jnp.float32),
+        ],
         scratch_shapes=[
             pltpu.VMEM(
                 (members * strips + regions, channels, local_members, rows, LANES), kind
@@ -374,11 +409,12 @@
             pltpu.VMEM((devices, width + EXTRAS, capacity), jnp.bfloat16),
             pltpu.VMEM((2, sources, width + EXTRAS, capacity), jnp.bfloat16),
             pltpu.VMEM((2,) + total, jnp.float32),
+            pltpu.VMEM((lower, 2 * width), jnp.bfloat16),
             pltpu.VMEM((bands * width, group * capacity), jnp.bfloat16),
         ]
         + [dma((units,)), dma((channels,)), dma((units, members))]
         + [dma((channels,))] * 2
-        + [dma((channels, members)), dma((5,)), dma((4,)), dma((3,))],
+        + [dma((channels, members)), dma((5,)), dma((4,)), dma((5,))],
         compiler_params=pltpu.CompilerParams(
             collective_id=0, has_side_effects=True, vmem_limit_bytes=60 << 20
         ),
@@ -386,20 +422,22 @@
             flops=1 << 34, bytes_accessed=4 * background.size, transcendentals=0
         ),
     )(background, ens_cols, *lines)
-    return out[0], list(out[1 : 1 + members]), out[1 + members], out[2 + members]
-
-
-def total_grams(near, far, bands):
-    width = near.shape[1] // 2
-    total = near + far
-    lower = bands * width // 2
-    gram = jnp.concatenate(
-        [
-            total[:lower, :width].reshape(bands // 2, width, width),
-            total[:lower, width:].reshape(bands // 2, width, width),
-        ]
+    return out[0], list(out[1 : 1 + members]), out[1 + members :]
+
+
+def total_grams(sums, bands):
+    near, far, edge = sums
+    lower, width = far.shape[0], far.shape[1] // 2
+    same = (
+        lax.broadcasted_iota(jnp.int32, (bands // 2, width, 2 * width), 1)
+        == lax.broadcasted_iota(jnp.int32, (bands // 2, width, 2 * width), 2) % width
     )
-    return gram, total[lower:, :width]
+    diagonal = edge[bands : bands + bands // 2][:, None, :]
+    other = far.astype(jnp.float32).reshape(bands // 2, width, 2 * width)
+    total = near[:lower].reshape(other.shape) + jnp.where(same, diagonal, other)
+    gram = jnp.concatenate([total[:, :, :width], total[:, :, width:]])
+    projected = near[lower : lower + bands] + edge[:bands]
+    return gram, projected[:, :width]
 
 
 def batched(left, right):
@@ -511,7 +549,6 @@
     slots, count, local_members, rows, lanes = part.shape
     strips = slots // members
     width = members * local_members
-    skip = (channels - count) // block
     return pl.pallas_call(
         functools.partial(apply_kernel, members),
         grid=(pl.cdiv(count, block),),
@@ -520,7 +557,7 @@
             pl.BlockSpec((slots, block, local_members, rows, lanes), lambda i: (0, i, 0, 0, 0)),
         ],
         out_specs=pl.BlockSpec(
-            (width, block, strips * rows, lanes), lambda i: (0, i + skip, 0, 0)
+            (width, block, strips * rows, lanes), lambda i: (0, i, 0, 0)
         ),
         out_shape=jax.ShapeDtypeStruct((width, channels, strips * rows, lanes), jnp.bfloat16),
         compiler_params=pltpu.CompilerParams(vmem_limit_bytes=32 << 20),
@@ -535,6 +572,7 @@
 def late_kernel(members, wide_ref, *refs):
     parts, (out_ref, done_ref, sem) = refs[:members], refs[members + 1 :]
     strips, block, _, rows, _ = parts[0].shape
+    first = out_ref.shape[1] - block
     copies = []
     for j in range(strips):
         for t in range(rows // TILE):
@@ -543,7 +581,7 @@
                 done_ref[k, :, c] = value
             copy = pltpu.make_async_copy(
                 done_ref.at[k],
-                out_ref.at[:, 0:block, pl.ds(j * rows + t * TILE, TILE), :],
+                out_ref.at[:, first : first + block, pl.ds(j * rows + t * TILE, TILE), :],
                 sem.at[k],
             )
             copy.start()
@@ -580,7 +618,7 @@
     slots, _, local_members, rows, lanes = recv.shape
     strips = slots // members
     width = members * local_members
-    states = jnp.concatenate([jnp.concatenate(late, axis=0), recv], axis=1)
+    states = jnp.concatenate([recv, jnp.concatenate(late, axis=0)], axis=1)
     channels = states.shape[1]
     states = states.reshape(members, strips, channels, local_members, rows, lanes)
     mean = jnp.sum(states, axis=(0, 3), dtype=jnp.float32) / width
@@ -609,15 +647,15 @@
         column.reshape(obs_rows // LANES, LANES)
         for column in (obs_value, obs_precision, obs_row, obs_patch[:, 0])
     ]
-    recv, late, near, far = exchange(background, obs_ens.T, lines, capacity)
-    for shift in range(1, members):
+    recv, late, sums = exchange(background, obs_ens.T, lines, capacity)
+    for shift in sorted(range(1, members), key=lambda g: (abs(2 * g - members), g)):
         ring = [(k, (k + shift) % members) for k in range(members)]
         late[shift] = lax.ppermute(late[shift], "member", ring)
-    transform = band_transforms(total_grams(near, far, lat_rows // BAND), width)
+    transform = band_transforms(total_grams(sums, lat_rows // BAND), width)
     if rows % TILE:
         return apply_plain(recv, late, transform, members)
     wide = widen(transform, members)
-    out = apply_early(recv, wide, members, channels, late[0].shape[1])
+    out = apply_early(recv, wide, members, channels, 2)
     return apply_late(late, wide, members, out)
 
 

time: 256 us -> 248 us (0.969)
  Pallas kernels: 225 us -> 199 us
  waiting for transfers between devices: 8.2 us -> 24.4 us
  local copies, waits for them, and re-layouts: 0.2 us -> 3.33 us
    pallas_call x1, Pallas kernels: 209 us -> 185 us  [exchange(): pl.pallas_call(functools.partial(exchange_kernel, members, regions, late)...]
    ppermute x3, waiting for transfers between devices: 8.2 us -> 24.4 us  [local(): late[shift] = lax.ppermute(late[shift], 'member', ring)]
    slice x2 -> x5, local copies, waits for them, and re-layouts: 0.18 us -> 3.32 us  [the longest x2 1.42 us: total_grams(): projected = near[lower:lower + bands] + edge[:bands]]
  transfers between devices with their start and end apart: 3 -> 3, of which waited for: 2 -> 2; matrix products, arithmetic and copies ran while one was open for 5% -> 6% of each run, Pallas kernels for 5% -> 4%
where the time goes in v3:
time: 248 us
  Pallas kernels  199 us (80%)
  waiting for transfers between devices  24.4 us (10%)
  matrix products  10.9 us (4%)
  starting transfers between devices  7.69 us (3%)
  local copies, waits for them, and re-layouts  3.33 us (1%)
    pallas_call x1, Pallas kernels, exchange(): pl.pallas_call(functools.partial(exchange_kernel, members, regions, late)...  185 us
    ppermute x3, waiting for transfers between devices, local(): late[shift] = lax.ppermute(late[shift], 'member', ring)  24.4 us
    dot_general x10, matrix products, batched(): jnp.einsum('bij,bjk->bik', left, right, precision=lax.Precision.HIGHEST)  9.62 us
    pallas_call x1, Pallas kernels, apply_early(): pl.pallas_call(functools.partial(apply_kernel, members), grid=(pl.cdiv(co...  7.77 us
    ppermute x3, starting transfers between devices, local(): late[shift] = lax.ppermute(late[shift], 'member', ring)  7.69 us
  transfers between devices with their start and end apart: 3, of which 2 were waited for; matrix products, arithmetic and copies ran while one was open for 6% of the time, Pallas kernels for 4%

profile of v3, /device:TPU:12, one launch (start us, length us, event | category | flops | bytes accessed | tf_op | source)
XLA Modules:
  0.0 247.8 jit_solution(14938515302347660467)
XLA Ops:
  0.0 185.1 %shard_map.64 = (bf16[8,10,16,24,128]{4,3,2,1,0:T(8,128)(2,1)}, bf16[2,3,16,24,128]{4,3,2,1,0:T(8,128)(2,1)}, bf16[2,3,16,24,128]{4,3,2,1,0:T(8,128)(2,1)}, bf16...) custom-call(bf16[16,13,24,1024]{3,2,1,0:T(8,128)(2,1)} %bg_ref.1, ...), custom_call_target="tpu_custom_call" | custom-call | flops 17179869184 | bytes 20447232 | tf_op jit(solution)/shard_map/pallas_call | solution.py:385
  185.1 3.3 %collective-permute-start = (bf16[2,3,16,24,128]{4,3,2,1,0:T(8,128)(2,1)}, bf16[2,3,16,24,128]{4,3,2,1,0:T(8,128)(2,1)S(1)}, u32[]{:S(2)}, u32[]{:S(2)}) collective-permute-start(bf16[2,3,16,24,128]{4,3,2,1,0:T(8,128)(2,1)} %get-tuple-element.17), channel_id=1, source_target_pairs={{0,8},{8,16},{16,24},{24,0},{1,9},{9,17},{17,25},{25,1},{2,10},{10... | collective-permute-start | bytes 1769480 | tf_op jit(solution)/shard_map/ppermute | solution.py:653
  188.4 4.4 %collective-permute-start.1 = (bf16[2,3,16,24,128]{4,3,2,1,0:T(8,128)(2,1)}, bf16[2,3,16,24,128]{4,3,2,1,0:T(8,128)(2,1)S(1)}, u32[]{:S(2)}, u32[]{:S(2)}) collective-permute-start(bf16[2,3,16,24,128]{4,3,2,1,0:T(8,128)(2,1)} %get-tuple-element.18), channel_id=1, source_target_pairs={{0,16},{8,24},{16,0},{24,8},{1,17},{9,25},{17,1},{25,9},{2,18},{10... | collective-permute-start | bytes 1769480 | tf_op jit(solution)/shard_map/ppermute | solution.py:653
  192.8 0.0 collective-permute-start.2
  192.8 0.7 slice.22
  193.5 0.7 slice.26
  194.2 0.7 slice.25
  194.9 1.0 slice.21
  196.0 1.0 fusion.6
  197.0 0.2 fusion.21
  197.1 0.3 multiply_reduce_fusion
  197.4 1.1 fusion.4
  198.6 1.1 fusion.2
  199.7 1.0 fusion.3
  200.7 0.9 fusion.22
  201.6 0.9 fusion.1
  202.5 0.9 fusion.23
  203.4 0.0 slice-start
  203.5 0.9 fusion.24
  204.4 0.9 fusion
  205.3 0.9 fusion.25
  206.2 0.9 convolution_divide_fusion
  207.1 0.0 slice-start.1
  207.2 1.3 fusion.26
  208.5 0.3 add_convert_fusion
  208.8 2.6 %shard_map.65.wide_ref = bf16[6,512,512]{2,1,0:T(8,128)(2,1)S(1)} custom-call(bf16[24,4,16,64]{3,2,1,0:T(8,128)(2,1)S(1)} %bitcast.34), custom_call_target="tpu_custom_call" | custom-call | flops 2147483648 | bytes 2097152 | tf_op jit(solution)/shard_map/pallas_call | solution.py:495
  211.4 0.0 slice-done
  211.4 7.8 %shard_map.66.refs_4_ = bf16[64,13,48,128]{3,2,1,0:T(8,128)(2,1)} custom-call(bf16[6,512,512]{2,1,0:T(8,128)(2,1)S(1)} %shard_map.65.wide_ref, bf16[8,10,16,24,128]{4,3,2,1,0:T(8,128)(2,1)S(1)} %bitcast.33), custom_call_target="tpu_custom_call" | custom-call | flops 4026531840 | bytes 15728640 | tf_op jit(solution)/shard_map/pallas_call | solution.py:552
  219.2 0.0 collective-permute-done.refs_1_
  219.2 20.8 %collective-permute-done.1.refs_2_ = bf16[2,3,16,24,128]{4,3,2,1,0:T(8,128)(2,1)S(1)} collective-permute-done((bf16[2,3,16,24,128]{4,3,2,1,0:T(8,128)(2,1)}, bf16[2,3,16,24,128]{4,3,2,1,0:T(8,128)(2,1)S(1)}, u32[]{:S(2)}, u32[]{:S(2)}) %collective-permute-start.1) | collective-permute-done | bytes 589856 | tf_op jit(solution)/shard_map/ppermute | solution.py:653
  240.0 3.7 %collective-permute-done.2.refs_3_ = bf16[2,3,16,24,128]{4,3,2,1,0:T(8,128)(2,1)S(1)} collective-permute-done((bf16[2,3,16,24,128]{4,3,2,1,0:T(8,128)(2,1)}, bf16[2,3,16,24,128]{4,3,2,1,0:T(8,128)(2,1)S(1)}, u32[]{:S(2)}, u32[]{:S(2)}) %collective-permute-start.2) | collective-permute-done | bytes 589856 | tf_op jit(solution)/shard_map/ppermute | solution.py:653
  243.7 4.0 %shard_map.67 = bf16[64,13,48,128]{3,2,1,0:T(8,128)(2,1)} custom-call(bf16[6,512,512]{2,1,0:T(8,128)(2,1)S(1)} %shard_map.65.wide_ref, bf16[2,3,16,24,128]{4,3,2,1,0:T(8,128)(2,1)S(1)} %copy-done, bf16[2,3,16,24,128]{4,3,2,1,0:T(8,128)(2,1)S(1)} %collective-permute-done.refs_1_, ...), custom_call_target="tpu_custom_call", output_to_operand_aliasing={{}: (5, {})} | custom-call | flops 1207959552 | bytes 4718592 | tf_op jit(solution)/shard_map/pallas_call | solution.py:597
  (9 shorter events, 0.0 us)
Async XLA Ops:
  185.1 34.1 %collective-permute-start = (bf16[2,3,16,24,128]{4,3,2,1,0:T(8,128)(2,1)}, bf16[2,3,16,24,128]{4,3,2,1,0:T(8,128)(2,1)S(1)}, u32[]{:S(2)}, u32[]{:S(2)}) collective-permute-start(bf16[2,3,16,24,128]{4,3,2,1,0:T(8,128)(2,1)} %get-tuple-element.17), channel_id=1, source_target_pairs={{0,8},{8,16},{16,24},{24,0},{1,9},{9,17},{17,25},{25,1},{2,10},{10... | collective-permute-start | bytes 1769480 | tf_op jit(solution)/shard_map/ppermute | solution.py:653
  188.4 51.6 %collective-permute-start.1 = (bf16[2,3,16,24,128]{4,3,2,1,0:T(8,128)(2,1)}, bf16[2,3,16,24,128]{4,3,2,1,0:T(8,128)(2,1)S(1)}, u32[]{:S(2)}, u32[]{:S(2)}) collective-permute-start(bf16[2,3,16,24,128]{4,3,2,1,0:T(8,128)(2,1)} %get-tuple-element.18), channel_id=1, source_target_pairs={{0,16},{8,24},{16,0},{24,8},{1,17},{9,25},{17,1},{25,9},{2,18},{10... | collective-permute-start | bytes 1769480 | tf_op jit(solution)/shard_map/ppermute | solution.py:653
  192.8 50.9 %collective-permute-start.2 = (bf16[2,3,16,24,128]{4,3,2,1,0:T(8,128)(2,1)}, bf16[2,3,16,24,128]{4,3,2,1,0:T(8,128)(2,1)S(1)}, u32[]{:S(2)}, u32[]{:S(2)}) collective-permute-start(bf16[2,3,16,24,128]{4,3,2,1,0:T(8,128)(2,1)} %get-tuple-element.19), channel_id=1, source_target_pairs={{0,24},{8,0},{16,8},{24,16},{1,25},{9,1},{17,9},{25,17},{2,26},{10... | collective-permute-start | bytes 1769480 | tf_op jit(solution)/shard_map/ppermute | solution.py:653
  203.4 8.0 %slice-start = ((s8[7864320]{0:T(1024)(128)(4,1)}), s8[4194304]{0:T(1024)(128)(4,1)S(1)}, s32[]{:S(2)}) async-start(s8[7864320]{0:T(1024)(128)(4,1)} %bitcast.32), calls=%async_computation | async-start | bytes 8388608
  207.1 4.3 %slice-start.1 = ((s8[7864320]{0:T(1024)(128)(4,1)}), s8[3670016]{0:T(1024)(128)(4,1)S(1)}, s32[]{:S(2)}) async-start(s8[7864320]{0:T(1024)(128)(4,1)} %bitcast.32), calls=%async_computation.1 | async-start | bytes 7340032
  211.4 32.2 %copy-start = (bf16[2,3,16,24,128]{4,3,2,1,0:T(8,128)(2,1)S(1)}, bf16[2,3,16,24,128]{4,3,2,1,0:T(8,128)(2,1)}, u32[]{:S(2)}) copy-start(bf16[2,3,16,24,128]{4,3,2,1,0:T(8,128)(2,1)} %get-tuple-element.16.refs_0_) | copy-start | bytes 1769476
